TPU v7x, 32 devices: a whole 2x2x4 slice. The times are simulated.
32 devices in a mesh: fsdp: 2 (over x), ctx: 16 (over z, y, core).
Axes of the slice: x: 2, y: 2, z: 4, core: 2. Of those that a mesh axis runs over, the one named last changes fastest.
Arguments:
- block_input: float32 [2, 2048, 1600], P('fsdp', 'ctx'), may hold values from -6 to 6
- attn_weight: bfloat16 [1600, 6400], P(None, ('fsdp', 'ctx')), may hold values from -4 to 4
- fc_weight: bfloat16 [1600, 6400], P(None, ('fsdp', 'ctx')), may hold values from -0.15625 to 0.15625
- down_weight: bfloat16 [1600, 6400], P(None, ('fsdp', 'ctx')), may hold values from -0.078125 to 0.078125
- vectors: bfloat16 [19200], P(('fsdp', 'ctx')), may hold values from -2.5 to 2
- cotangent: float32 [2, 2048, 1600], P('fsdp', 'ctx'), may hold values from -6 to 6
Outputs:
- block_output: float32 [2, 2048, 1600], P('fsdp', 'ctx')
- input_grad: float32 [2, 2048, 1600], P('fsdp', 'ctx')
- attn_grad: float32 [1600, 6400], P(None, ('fsdp', 'ctx'))
- fc_grad: float32 [1600, 6400], P(None, ('fsdp', 'ctx'))
- down_grad: float32 [1600, 6400], P(None, ('fsdp', 'ctx'))
- vector_grad: float32 [19200], P(('fsdp', 'ctx'))
All inputs are finite; a program needn't handle non-finite values.
Results may differ from a plain program's by a relative error of at most 0.01.
Values may be sent and summed in bfloat16 or wider, within the bound.
A program may use at most 512 MiB of HBM per device.

v0:
```python
import math

import jax
import jax.numpy as jnp
from jax import lax
from jax.sharding import PartitionSpec as P

D = 1600
HEADS = 25
HEAD_DIM = 64


epsilon = 1e-05
gelu_coeff = 0.7978845608028654


def shifted(shard, axis, by):
    size = lax.axis_size(axis)
    return lax.ppermute(shard, axis, [(i, (i + by) % size) for i in range(size)])


def layer_norm(values, gain_vec, shift_vec):
    center = values - jnp.mean(values, axis=-1, keepdims=True)
    spread = jnp.mean(center * center, axis=-1, keepdims=True)
    return center * lax.rsqrt(spread + epsilon) * gain_vec + shift_vec


def gelu_tanh(values):
    return (
        0.5 * values * (1.0 + jnp.tanh(gelu_coeff * (values + 0.044715 * values * values * values)))
    )


def block_rows(row_count):
    pieces = 1
    while row_count % pieces or row_count // pieces > 1024:
        pieces += 1
    return row_count // pieces


def keep_same(current):
    return current


def fetch_weights(members):
    return (
        lax.all_gather(members[0], ("fsdp", "ctx"), axis=1, tiled=True),
        lax.all_gather(members[1], ("fsdp", "ctx"), axis=1, tiled=True),
    )


def contract_rows(left_side, right_side):
    return lax.dot_general(
        left_side, right_side, (((0,), (0,)), ((), ())), preferred_element_type=jnp.float32
    )


def contract_cols(left_side, right_side):
    return lax.dot_general(
        left_side, right_side, (((1,), (1,)), ((), ())), preferred_element_type=jnp.float32
    )


def pair_grads(
    query_heads,
    d_mixed_heads,
    log_total,
    delta_sum,
    key_heads,
    value_heads,
    query_pos,
    key_pos,
    score_scale,
):
    scores = (
        jnp.einsum("qhd,khd->hqk", query_heads, key_heads, preferred_element_type=jnp.float32)
        * score_scale
    )
    allowed = key_pos[None, :] <= query_pos[:, None]
    scores = jnp.where(allowed[None], scores, -jnp.inf)
    probs = jnp.exp(scores - log_total[:, :, None])
    probs_low = probs.astype(jnp.bfloat16)
    d_values_part = jnp.einsum(
        "hqk,qhd->khd", probs_low, d_mixed_heads, preferred_element_type=jnp.float32
    )
    d_probs = jnp.einsum(
        "qhd,khd->hqk", d_mixed_heads, value_heads, preferred_element_type=jnp.float32
    )
    d_scores = (probs * (d_probs - delta_sum[:, :, None]) * score_scale).astype(jnp.bfloat16)
    d_query_part = jnp.einsum(
        "hqk,khd->qhd", d_scores, key_heads, preferred_element_type=jnp.float32
    )
    d_key_part = jnp.einsum(
        "hqk,qhd->khd", d_scores, query_heads, preferred_element_type=jnp.float32
    )
    return (d_query_part, d_key_part, d_values_part)


def per_device(block_input, attn_weight, fc_weight, down_weight, vectors, cotangent):
    ctx_devices = lax.axis_size("ctx")
    ctx_place = lax.axis_index("ctx")
    inputs = block_input[0]
    grad_output = cotangent[0]
    row_count = inputs.shape[0]
    score_scale = 1.0 / math.sqrt(HEAD_DIM)
    attn_full, vector_full = fetch_weights((attn_weight, vectors.reshape(1, -1)))
    vector_full = vector_full.reshape(-1).astype(jnp.float32)
    gain_one = vector_full[0:D]
    shift_one = vector_full[D : 2 * D]
    bias_query = vector_full[2 * D : 3 * D]
    bias_value = vector_full[3 * D : 4 * D]
    bias_out = vector_full[4 * D : 5 * D]
    gain_two = vector_full[5 * D : 6 * D]
    shift_two = vector_full[6 * D : 7 * D]
    bias_proj = vector_full[7 * D : 8 * D]
    fc_bias = vector_full[8 * D : 12 * D]
    normed_one, pull_one = jax.vjp(layer_norm, inputs, gain_one, shift_one)
    normed_low = normed_one.astype(jnp.bfloat16)
    projected = jnp.dot(normed_low, attn_full[:, 0 : 3 * D], preferred_element_type=jnp.float32)
    queries = (projected[:, 0:D] + bias_query).astype(jnp.bfloat16)
    keys_own = projected[:, D : 2 * D].astype(jnp.bfloat16)
    values_own = (projected[:, 2 * D : 3 * D] + bias_value).astype(jnp.bfloat16)
    query_heads = queries.reshape(row_count, HEADS, HEAD_DIM)
    query_pos = ctx_place * row_count + jnp.arange(row_count, dtype=jnp.int32)
    last_query = ctx_place * row_count + row_count - 1
    initial = (
        jnp.full((HEADS, row_count), -1e30, jnp.float32),
        jnp.zeros((HEADS, row_count), jnp.float32),
        jnp.zeros((row_count, HEADS, HEAD_DIM), jnp.float32),
    )
    running = initial
    keys_piece = lax.all_gather(keys_own, "ctx", axis=0, tiled=True)
    values_piece = lax.all_gather(values_own, "ctx", axis=0, tiled=True)
    piece_rows = keys_piece.shape[0]
    block_size = block_rows(piece_rows)
    block_count = piece_rows // block_size
    key_blocks = keys_piece.reshape(block_count, block_size, HEADS, HEAD_DIM)
    value_blocks = values_piece.reshape(block_count, block_size, HEADS, HEAD_DIM)
    block_starts = block_size * jnp.arange(block_count, dtype=jnp.int32)

    def one_block(state_in, inputs_blk):
        key_blk, value_blk, first_key = inputs_blk

        def visit(current):
            run_max, run_total, accum = current
            scores = (
                jnp.einsum("qhd,khd->hqk", query_heads, key_blk, preferred_element_type=jnp.float32)
                * score_scale
            )
            key_pos = first_key + jnp.arange(block_size, dtype=jnp.int32)
            allowed = key_pos[None, :] <= query_pos[:, None]
            scores = jnp.where(allowed[None], scores, -jnp.inf)
            new_max = jnp.maximum(run_max, jnp.max(scores, axis=-1))
            weights = jnp.exp(scores - new_max[:, :, None])
            factor = jnp.exp(run_max - new_max)
            run_total = run_total * factor + jnp.sum(weights, axis=-1)
            accum = accum * jnp.transpose(factor)[:, :, None] + jnp.einsum(
                "hqk,khd->qhd",
                weights.astype(jnp.bfloat16),
                value_blk,
                preferred_element_type=jnp.float32,
            )
            return (new_max, run_total, accum)

        return (lax.cond(first_key <= last_query, visit, keep_same, state_in), None)

    running, unused = lax.scan(one_block, running, (key_blocks, value_blocks, block_starts))
    run_max, run_total, accum = running
    attended = accum / jnp.transpose(run_total)[:, :, None]
    log_total = run_max + jnp.log(run_total)
    mixed_low = attended.reshape(row_count, D).astype(jnp.bfloat16)
    middle = (
        inputs
        + jnp.dot(mixed_low, attn_full[:, 3 * D : 4 * D], preferred_element_type=jnp.float32)
        + bias_out
    )
    fc_full, down_full = fetch_weights((fc_weight, down_weight))
    normed_two, pull_two = jax.vjp(layer_norm, middle, gain_two, shift_two)
    normed_two_low = normed_two.astype(jnp.bfloat16)
    pre_act = jnp.dot(normed_two_low, fc_full, preferred_element_type=jnp.float32) + fc_bias
    activated, pull_gelu = jax.vjp(gelu_tanh, pre_act)
    act_low = activated.astype(jnp.bfloat16)
    block_output = middle + contract_cols(act_low, down_full) + bias_proj
    grad_low = grad_output.astype(jnp.bfloat16)
    d_act = jnp.dot(grad_low, down_full, preferred_element_type=jnp.float32)
    d_pre = pull_gelu(d_act)[0]
    d_pre_low = d_pre.astype(jnp.bfloat16)
    d_normed_two = contract_cols(d_pre_low, fc_full)
    d_middle_norm, grad_gain_two, grad_shift_two = pull_two(d_normed_two)
    d_middle = grad_output + d_middle_norm
    d_middle_low = d_middle.astype(jnp.bfloat16)
    d_mixed = contract_cols(d_middle_low, attn_full[:, 3 * D : 4 * D])
    d_mixed_heads = d_mixed.astype(jnp.bfloat16).reshape(row_count, HEADS, HEAD_DIM)
    mixed_heads = mixed_low.reshape(row_count, HEADS, HEAD_DIM)
    delta_sum = jnp.einsum(
        "qhd,qhd->hq", d_mixed_heads, mixed_heads, preferred_element_type=jnp.float32
    )
    zero_rows = jnp.zeros((row_count, D), jnp.float32)
    zero_heads = jnp.zeros((row_count, HEADS, HEAD_DIM), jnp.float32)
    key_heads_own = keys_own.reshape(row_count, HEADS, HEAD_DIM)
    value_heads_own = values_own.reshape(row_count, HEADS, HEAD_DIM)

    def one_pass(turn_index, running):
        queries_held, d_mixed_held, d_queries_held, lse_held, delta_held, d_keys, d_values = running
        anchor = (ctx_place - turn_index) % ctx_devices

        def visit(sums_in):
            d_queries_in, d_keys_in, d_values_in = sums_in
            held_pos = anchor * row_count + jnp.arange(row_count, dtype=jnp.int32)
            d_query_part, d_key_part, d_value_part = pair_grads(
                queries_held,
                d_mixed_held,
                lse_held,
                delta_held,
                key_heads_own,
                value_heads_own,
                held_pos,
                query_pos,
                score_scale,
            )
            return (
                d_queries_in + d_query_part,
                d_keys_in + d_key_part.reshape(row_count, D),
                d_values_in + d_value_part.reshape(row_count, D),
            )

        d_queries_held, d_keys, d_values = lax.cond(
            anchor >= ctx_place, visit, keep_same, (d_queries_held, d_keys, d_values)
        )
        queries_held, d_mixed_held = shifted((queries_held, d_mixed_held), "ctx", 1)
        d_queries_held, lse_held, delta_held = shifted(
            (d_queries_held, lse_held, delta_held), "ctx", 1
        )
        return (queries_held, d_mixed_held, d_queries_held, lse_held, delta_held, d_keys, d_values)

    final_state = lax.fori_loop(
        0,
        ctx_devices,
        one_pass,
        (query_heads, d_mixed_heads, zero_heads, log_total, delta_sum, zero_rows, zero_rows),
    )
    d_queries = final_state[2].reshape(row_count, D)
    d_keys = final_state[5]
    d_values = final_state[6]
    d_projected_low = jnp.concatenate([d_queries, d_keys, d_values], axis=1).astype(jnp.bfloat16)
    d_normed_one = contract_cols(d_projected_low, attn_full[:, 0 : 3 * D])
    d_input_norm, grad_gain_one, grad_shift_one = pull_one(d_normed_one)
    input_grad = d_middle + d_input_norm
    attn_right = jnp.concatenate([d_projected_low, d_middle_low], axis=1)
    attn_cols, fc_cols, down_cols = (
        lax.all_to_all(attn_right, ("fsdp", "ctx"), split_axis=1, concat_axis=0, tiled=True),
        lax.all_to_all(d_pre_low, ("fsdp", "ctx"), split_axis=1, concat_axis=0, tiled=True),
        lax.all_to_all(act_low, ("fsdp", "ctx"), split_axis=1, concat_axis=0, tiled=True),
    )
    shard_cols = attn_weight.shape[1]
    global_cols = lax.axis_index(("fsdp", "ctx")) * shard_cols + jnp.arange(
        shard_cols, dtype=jnp.int32
    )
    qkv_column = (global_cols < 3 * D)[None, :]
    normed_piece = lax.all_gather(normed_low, ("fsdp", "ctx"), axis=0, tiled=True)
    mixed_piece = lax.all_gather(mixed_low, ("fsdp", "ctx"), axis=0, tiled=True)
    normed_two_piece = lax.all_gather(normed_two_low, ("fsdp", "ctx"), axis=0, tiled=True)
    grad_piece = lax.all_gather(grad_low, ("fsdp", "ctx"), axis=0, tiled=True)
    attn_term = jnp.where(
        qkv_column, contract_rows(normed_piece, attn_cols), contract_rows(mixed_piece, attn_cols)
    )
    fc_shard = contract_rows(normed_two_piece, fc_cols)
    down_shard = contract_rows(grad_piece, down_cols)
    grad_vectors = jnp.concatenate(
        [
            grad_gain_one,
            grad_shift_one,
            jnp.sum(d_queries, axis=0),
            jnp.sum(d_values, axis=0),
            jnp.sum(d_middle, axis=0),
            grad_gain_two,
            grad_shift_two,
            jnp.sum(grad_output, axis=0),
            jnp.sum(d_pre, axis=0),
        ]
    )
    vector_shard = lax.psum_scatter(
        grad_vectors[None, :], ("fsdp", "ctx"), scatter_dimension=1, tiled=True
    )
    return (
        block_output[None],
        input_grad[None],
        attn_term,
        fc_shard,
        down_shard,
        vector_shard.reshape(-1),
    )


def solution(mesh):
    return jax.shard_map(
        per_device,
        mesh=mesh,
        in_specs=(
            P("fsdp", "ctx", None),
            P(None, ("fsdp", "ctx")),
            P(None, ("fsdp", "ctx")),
            P(None, ("fsdp", "ctx")),
            P(("fsdp", "ctx")),
            P("fsdp", "ctx", None),
        ),
        out_specs=(
            P("fsdp", "ctx", None),
            P("fsdp", "ctx", None),
            P(None, ("fsdp", "ctx")),
            P(None, ("fsdp", "ctx")),
            P(None, ("fsdp", "ctx")),
            P(("fsdp", "ctx")),
        ),
        check_vma=False,
    )
```

profile of v0, /device:TPU:31, one launch (start us, length us, event | category | flops | bytes accessed | tf_op | source)
XLA Modules:
  0.0 1757.7 jit_solution(13935481590268661602)
XLA Ops:
  8.8 40.1 %all-reduce = bf16[19200]{0:T(1024)(128)(2,1)S(1)} all-reduce(bf16[19200]{0:T(1024)(128)(2,1)S(1)} %dynamic-update-slice), channel_id=2, replica_groups=mesh['fsdp'=2,'ctx'=16] {'fsdp','ctx'}, use_global_device_ids=true, to_apply=%add | all-reduce | flops 19200 | bytes 76800
  54.2 92.2 %all-gather.11.cloned.1.call-done = bf16[1600,6400]{0,1:T(8,128)(2,1)} async-done(((bf16[1600,200]{0,1:T(8,128)(2,1)}), bf16[1600,6400]{0,1:T(8,128)(2,1)}) %all-gather.11.cloned.1.call-update) | async-done | bytes 20480016 | tf_op jit(solution)/shard_map/all_gather | solution.py:47
  161.9 60.1 %all-gather.15.cloned.1.call-done = bf16[2048,1600]{0,1:T(8,128)(2,1)} async-done(((bf16[128,1600]{0,1:T(8,128)(2,1)}), bf16[2048,1600]{0,1:T(8,128)(2,1)}) %all-gather.15.cloned.1.call-update) | async-done | bytes 6553616 | tf_op jit(solution)/shard_map/all_gather | solution.py:133
  222.0 15.6 reshape.215
  245.5 44.3 %all-gather.13.cloned.1.call-done = bf16[2048,1600]{0,1:T(8,128)(2,1)} async-done(((bf16[128,1600]{0,1:T(8,128)(2,1)}), bf16[2048,1600]{0,1:T(8,128)(2,1)}) %all-gather.13.cloned.1.call-update) | async-done | bytes 6553616 | tf_op jit(solution)/shard_map/all_gather | solution.py:132
  289.8 15.6 reshape.213
  313.3 27.0 %while.43 = (s32[]{:T(128)}, f32[25,128]{1,0:T(8,128)S(1)}, f32[25,128]{1,0:T(8,128)S(1)}, f32[128,25,64]{0,2,1:T(8,128)S(1)}, s32[2]{0:T(128)S(1)}, /*index=5*/...) while((s32[]{:T(128)}, f32[25,128]{1,0:T(8,128)S(1)}, ...), condition=%wide.region_7.8_spmd.clone, body=%wide.region_2.7_spmd.clone.sunk | while | flops 862349824 | bytes 48401688 | solution.py:167
  314.8 12.1 conditional.6
  328.1 12.1 conditional.6
  345.4 80.8 %all-gather.17.cloned.1.call-done = bf16[1600,6400]{0,1:T(8,128)(2,1)} async-done(((bf16[1600,200]{0,1:T(8,128)(2,1)}), bf16[1600,6400]{0,1:T(8,128)(2,1)}) %all-gather.17.cloned.1.call-update) | async-done | bytes 20480016 | tf_op jit(solution)/shard_map/all_gather | solution.py:47
  426.2 11.7 convolution_add_fusion
  437.9 124.7 %all-gather.19.cloned.1.call-done = bf16[1600,6400]{0,1:T(8,128)(2,1)} async-done(((bf16[1600,200]{0,1:T(8,128)(2,1)}), bf16[1600,6400]{0,1:T(8,128)(2,1)}) %all-gather.19.cloned.1.call-update) | async-done | bytes 20480016 | tf_op jit(solution)/shard_map/all_gather | solution.py:48
  562.6 13.2 fusion.78
  575.8 14.3 fusion.76
  601.2 489.2 %while.44 = (s32[]{:T(128)}, bf16[128,25,64]{0,2,1:T(8,128)(2,1)S(1)}, bf16[128,25,64]{0,2,1:T(8,128)(2,1)}, f32[128,25,64]{0,2,1:T(8,128)}, f32[25,128]{1,0:T(8...) while((s32[]{:T(128)}, ...), condition=%wide.region_15.16_spmd.clone, body=%wide.region_12.15_spmd.clone.sunk | while | flops 266051856 | bytes 36670180 | solution.py:236
  1093.4 11.1 fusion.77
  1122.4 32.8 %all-to-all-done = bf16[128,32,200]{0,2,1:T(8,128)(2,1)} async-done(((bf16[128,32,200]{0,2,1:T(8,128)(2,1)}), bf16[128,32,200]{0,2,1:T(8,128)(2,1)}, u32[]{:S(2)}, u32[]{:S(2)}) %all-to-all-start) | async-done | bytes 1638432 | tf_op jit(solution)/shard_map/all_to_all | solution.py:251
  1168.2 31.0 %all-to-all-done.2 = bf16[128,32,200]{0,2,1:T(8,128)(2,1)} async-done(((bf16[128,32,200]{0,2,1:T(8,128)(2,1)}), bf16[128,32,200]{0,2,1:T(8,128)(2,1)}, u32[]{:S(2)}, u32[]{:S(2)}) %all-to-all-start.2) | async-done | bytes 1638432 | tf_op jit(solution)/shard_map/all_to_all | solution.py:253
  1208.2 12.5 fusion.49
  1223.1 21.4 %all-reduce.4.cloned.1.call-done = f32[1,19200]{1,0:T(1,128)} async-done(((f32[1,19200]{1,0:T(1,128)}), f32[1,19200]{1,0:T(1,128)}) %all-reduce.4.cloned.1.call-update) | async-done | bytes 76816
  1245.8 123.6 %all-gather.27.cloned.1.call-done = bf16[4096,1600]{0,1:T(8,128)(2,1)} async-done(((bf16[128,1600]{0,1:T(8,128)(2,1)}), bf16[4096,1600]{0,1:T(8,128)(2,1)}) %all-gather.27.cloned.1.call-update) | async-done | bytes 13107216 | tf_op jit(solution)/shard_map/all_gather | solution.py:263
  1380.2 112.8 %all-gather.21.cloned.1.call-done = bf16[4096,1600]{0,1:T(8,128)(2,1)} async-done(((bf16[128,1600]{0,1:T(8,128)(2,1)}), bf16[4096,1600]{0,1:T(8,128)(2,1)}) %all-gather.21.cloned.1.call-update) | async-done | bytes 13107216 | tf_op jit(solution)/shard_map/all_gather | solution.py:260
  1502.6 113.9 %all-gather.25.cloned.1.call-done = bf16[4096,1600]{0,1:T(8,128)(2,1)} async-done(((bf16[128,1600]{0,1:T(8,128)(2,1)}), bf16[4096,1600]{0,1:T(8,128)(2,1)}) %all-gather.25.cloned.1.call-update) | async-done | bytes 13107216 | tf_op jit(solution)/shard_map/all_gather | solution.py:262
  1627.2 112.7 %all-gather.23.cloned.1.call-done = bf16[4096,1600]{0,1:T(8,128)(2,1)} async-done(((bf16[128,1600]{0,1:T(8,128)(2,1)}), bf16[4096,1600]{0,1:T(8,128)(2,1)}) %all-gather.23.cloned.1.call-update) | async-done | bytes 13107216 | tf_op jit(solution)/shard_map/all_gather | solution.py:261
  (445 shorter events, 661.7 us)
Async XLA Ops:
  7.2 139.2 %all-gather.11.cloned.1.call-start = ((), (), s32[]{:S(2)}) async-start(), calls=%async_computation.3 | async-start | bytes 21964800 | tf_op jit(solution)/shard_map/all_gather | solution.py:47
  7.9 214.1 %all-gather.15.cloned.1.call-start = ((), (), s32[]{:S(2)}) async-start(), calls=%async_computation.5 | async-start | bytes 6963200 | tf_op jit(solution)/shard_map/all_gather | solution.py:133
  156.9 132.9 %all-gather.13.cloned.1.call-start = ((), (), s32[]{:S(2)}) async-start(), calls=%async_computation.4 | async-start | bytes 6963200 | tf_op jit(solution)/shard_map/all_gather | solution.py:132
  158.9 267.3 %all-gather.17.cloned.1.call-start = ((), (), s32[]{:S(2)}) async-start(), calls=%async_computation.6 | async-start | bytes 21964800 | tf_op jit(solution)/shard_map/all_gather | solution.py:47
  159.5 403.1 %all-gather.19.cloned.1.call-start = ((), (), s32[]{:S(2)}) async-start(), calls=%async_computation.7 | async-start | bytes 21964800 | tf_op jit(solution)/shard_map/all_gather | solution.py:48
  160.1 1084.4 %all-reduce.4.cloned.1.call-start = ((), (), s32[]{:S(2)}) async-start(), calls=%async_computation.12 | async-start | bytes 153600
  631.0 20.6 %collective-permute-start.2 = (f32[128,25,64]{0,2,1:T(8,128)}, f32[128,25,64]{0,2,1:T(8,128)}, u32[]{:S(2)}, u32[]{:S(2)}) collective-permute-start(f32[128,25,64]{0,2,1:T(8,128)} %get-tuple-element.811), channel_id=1, source_target_pairs={{0,1},{1,2},{2,3},{3,4},{4,5},{5,6},{6,7},{7,8},{8,9},{9,10},{10,1... | collective-permute-start | bytes 2457608 | tf_op jit(solution)/shard_map/while/body/eval_jaxpr/ppermute | solution.py:19
  661.7 20.6 %collective-permute-start.2 = (f32[128,25,64]{0,2,1:T(8,128)}, f32[128,25,64]{0,2,1:T(8,128)}, u32[]{:S(2)}, u32[]{:S(2)}) collective-permute-start(f32[128,25,64]{0,2,1:T(8,128)} %get-tuple-element.811), channel_id=1, source_target_pairs={{0,1},{1,2},{2,3},{3,4},{4,5},{5,6},{6,7},{7,8},{8,9},{9,10},{10,1... | collective-permute-start | bytes 2457608 | tf_op jit(solution)/shard_map/while/body/eval_jaxpr/ppermute | solution.py:19
  692.4 20.6 %collective-permute-start.2 = (f32[128,25,64]{0,2,1:T(8,128)}, f32[128,25,64]{0,2,1:T(8,128)}, u32[]{:S(2)}, u32[]{:S(2)}) collective-permute-start(f32[128,25,64]{0,2,1:T(8,128)} %get-tuple-element.811), channel_id=1, source_target_pairs={{0,1},{1,2},{2,3},{3,4},{4,5},{5,6},{6,7},{7,8},{8,9},{9,10},{10,1... | collective-permute-start | bytes 2457608 | tf_op jit(solution)/shard_map/while/body/eval_jaxpr/ppermute | solution.py:19
  723.1 20.6 %collective-permute-start.2 = (f32[128,25,64]{0,2,1:T(8,128)}, f32[128,25,64]{0,2,1:T(8,128)}, u32[]{:S(2)}, u32[]{:S(2)}) collective-permute-start(f32[128,25,64]{0,2,1:T(8,128)} %get-tuple-element.811), channel_id=1, source_target_pairs={{0,1},{1,2},{2,3},{3,4},{4,5},{5,6},{6,7},{7,8},{8,9},{9,10},{10,1... | collective-permute-start | bytes 2457608 | tf_op jit(solution)/shard_map/while/body/eval_jaxpr/ppermute | solution.py:19
  753.8 20.6 %collective-permute-start.2 = (f32[128,25,64]{0,2,1:T(8,128)}, f32[128,25,64]{0,2,1:T(8,128)}, u32[]{:S(2)}, u32[]{:S(2)}) collective-permute-start(f32[128,25,64]{0,2,1:T(8,128)} %get-tuple-element.811), channel_id=1, source_target_pairs={{0,1},{1,2},{2,3},{3,4},{4,5},{5,6},{6,7},{7,8},{8,9},{9,10},{10,1... | collective-permute-start | bytes 2457608 | tf_op jit(solution)/shard_map/while/body/eval_jaxpr/ppermute | solution.py:19
  784.5 20.6 %collective-permute-start.2 = (f32[128,25,64]{0,2,1:T(8,128)}, f32[128,25,64]{0,2,1:T(8,128)}, u32[]{:S(2)}, u32[]{:S(2)}) collective-permute-start(f32[128,25,64]{0,2,1:T(8,128)} %get-tuple-element.811), channel_id=1, source_target_pairs={{0,1},{1,2},{2,3},{3,4},{4,5},{5,6},{6,7},{7,8},{8,9},{9,10},{10,1... | collective-permute-start | bytes 2457608 | tf_op jit(solution)/shard_map/while/body/eval_jaxpr/ppermute | solution.py:19
  815.2 20.6 %collective-permute-start.2 = (f32[128,25,64]{0,2,1:T(8,128)}, f32[128,25,64]{0,2,1:T(8,128)}, u32[]{:S(2)}, u32[]{:S(2)}) collective-permute-start(f32[128,25,64]{0,2,1:T(8,128)} %get-tuple-element.811), channel_id=1, source_target_pairs={{0,1},{1,2},{2,3},{3,4},{4,5},{5,6},{6,7},{7,8},{8,9},{9,10},{10,1... | collective-permute-start | bytes 2457608 | tf_op jit(solution)/shard_map/while/body/eval_jaxpr/ppermute | solution.py:19
  845.9 20.6 %collective-permute-start.2 = (f32[128,25,64]{0,2,1:T(8,128)}, f32[128,25,64]{0,2,1:T(8,128)}, u32[]{:S(2)}, u32[]{:S(2)}) collective-permute-start(f32[128,25,64]{0,2,1:T(8,128)} %get-tuple-element.811), channel_id=1, source_target_pairs={{0,1},{1,2},{2,3},{3,4},{4,5},{5,6},{6,7},{7,8},{8,9},{9,10},{10,1... | collective-permute-start | bytes 2457608 | tf_op jit(solution)/shard_map/while/body/eval_jaxpr/ppermute | solution.py:19
  876.6 20.6 %collective-permute-start.2 = (f32[128,25,64]{0,2,1:T(8,128)}, f32[128,25,64]{0,2,1:T(8,128)}, u32[]{:S(2)}, u32[]{:S(2)}) collective-permute-start(f32[128,25,64]{0,2,1:T(8,128)} %get-tuple-element.811), channel_id=1, source_target_pairs={{0,1},{1,2},{2,3},{3,4},{4,5},{5,6},{6,7},{7,8},{8,9},{9,10},{10,1... | collective-permute-start | bytes 2457608 | tf_op jit(solution)/shard_map/while/body/eval_jaxpr/ppermute | solution.py:19
  907.3 20.6 %collective-permute-start.2 = (f32[128,25,64]{0,2,1:T(8,128)}, f32[128,25,64]{0,2,1:T(8,128)}, u32[]{:S(2)}, u32[]{:S(2)}) collective-permute-start(f32[128,25,64]{0,2,1:T(8,128)} %get-tuple-element.811), channel_id=1, source_target_pairs={{0,1},{1,2},{2,3},{3,4},{4,5},{5,6},{6,7},{7,8},{8,9},{9,10},{10,1... | collective-permute-start | bytes 2457608 | tf_op jit(solution)/shard_map/while/body/eval_jaxpr/ppermute | solution.py:19
  938.0 20.6 %collective-permute-start.2 = (f32[128,25,64]{0,2,1:T(8,128)}, f32[128,25,64]{0,2,1:T(8,128)}, u32[]{:S(2)}, u32[]{:S(2)}) collective-permute-start(f32[128,25,64]{0,2,1:T(8,128)} %get-tuple-element.811), channel_id=1, source_target_pairs={{0,1},{1,2},{2,3},{3,4},{4,5},{5,6},{6,7},{7,8},{8,9},{9,10},{10,1... | collective-permute-start | bytes 2457608 | tf_op jit(solution)/shard_map/while/body/eval_jaxpr/ppermute | solution.py:19
  1106.0 263.4 %all-gather.27.cloned.1.call-start = ((), (), s32[]{:S(2)}) async-start(), calls=%async_computation.11 | async-start | bytes 13516800 | tf_op jit(solution)/shard_map/all_gather | solution.py:263
  1106.8 386.2 %all-gather.21.cloned.1.call-start = ((), (), s32[]{:S(2)}) async-start(), calls=%async_computation.8 | async-start | bytes 13516800 | tf_op jit(solution)/shard_map/all_gather | solution.py:260
  1107.5 509.0 %all-gather.25.cloned.1.call-start = ((), (), s32[]{:S(2)}) async-start(), calls=%async_computation.10 | async-start | bytes 13516800 | tf_op jit(solution)/shard_map/all_gather | solution.py:262
  1108.3 631.6 %all-gather.23.cloned.1.call-start = ((), (), s32[]{:S(2)}) async-start(), calls=%async_computation.9 | async-start | bytes 13516800 | tf_op jit(solution)/shard_map/all_gather | solution.py:261
  1111.5 43.7 %all-to-all-start = ((bf16[128,32,200]{0,2,1:T(8,128)(2,1)}), bf16[128,32,200]{0,2,1:T(8,128)(2,1)}, u32[]{:S(2)}, u32[]{:S(2)}) async-start(bf16[128,32,200]{0,2,1:T(8,128)(2,1)} %bitcast.141), calls=%async_computation | async-start | bytes 3276800 | tf_op jit(solution)/shard_map/all_to_all | solution.py:251
  1155.1 44.0 %all-to-all-start.2 = ((bf16[128,32,200]{0,2,1:T(8,128)(2,1)}), bf16[128,32,200]{0,2,1:T(8,128)(2,1)}, u32[]{:S(2)}, u32[]{:S(2)}) async-start(bf16[128,32,200]{0,2,1:T(8,128)(2,1)} %bitcast.140), calls=%async_computation.2 | async-start | bytes 3276800 | tf_op jit(solution)/shard_map/all_to_all | solution.py:253
  1199.2 303.4 %all-to-all-start.1 = ((bf16[128,32,200]{0,2,1:T(8,128)(2,1)}), bf16[128,32,200]{0,2,1:T(8,128)(2,1)}, u32[]{:S(2)}, u32[]{:S(2)}) async-start(bf16[128,32,200]{0,2,1:T(8,128)(2,1)} %bitcast.139), calls=%async_computation.1 | async-start | bytes 3276800 | tf_op jit(solution)/shard_map/all_to_all | solution.py:252
  (100 other events, 2546.7 us)
Sparse Core Ops, SparseCore 0:
  10.9 135.4 all-gather.10
  157.0 64.9 all-gather.14
  224.8 64.9 all-gather.12
  292.6 133.5 all-gather.16
  428.9 133.5 all-gather.18
  1106.1 138.3 all-reduce.3
  1247.3 122.0 all-gather.26
  1372.3 120.6 all-gather.20
  1495.8 120.6 all-gather.24
  1619.2 120.6 all-gather.22
where the time goes:
time: 1770 us; the launch traced here: 1760 us
  waiting for transfers between devices  1220 us (69%)
  starting transfers between devices  199 us (11%)
  matrix products  144 us (8%)
  local copies, waits for them, and re-layouts  115 us (6%)
  blocking collectives  40.1 us (2%)
  other arithmetic  25.9 us (1%)
    ppermute x80, waiting for transfers between devices, shifted(): lax.ppermute(shard, axis, [(i, (i + by) % size) for i in range(size)])  260 us
    all_gather x2, waiting for transfers between devices, fetch_weights(): lax.all_gather(members[0], ('fsdp', 'ctx'), axis=1, tiled=True)  173 us
    ppermute x80, starting transfers between devices, shifted(): lax.ppermute(shard, axis, [(i, (i + by) % size) for i in range(size)])  172 us
    all_gather x1, waiting for transfers between devices, fetch_weights(): lax.all_gather(members[1], ('fsdp', 'ctx'), axis=1, tiled=True)  125 us
    all_gather x1, waiting for transfers between devices, per_device(): grad_piece = lax.all_gather(grad_low, ('fsdp', 'ctx'), axis=0, tiled=True)  124 us
    all_gather x1, waiting for transfers between devices, per_device(): lax.all_gather(normed_two_low, ('fsdp', 'ctx'), axis=0, tiled=True)  114 us
    all_gather x1, waiting for transfers between devices, per_device(): lax.all_gather(normed_low, ('fsdp', 'ctx'), axis=0, tiled=True)  113 us
    all_gather x1, waiting for transfers between devices, per_device(): mixed_piece = lax.all_gather(mixed_low, ('fsdp', 'ctx'), axis=0, tiled=True)  113 us
  transfers between devices with their start and end apart: 93, of which 60 were waited for; matrix products, arithmetic and copies ran while one was open for 11% of the time, Pallas kernels for 0%

commit v1 on v0

v1 whole, which is shorter than its diff:
```python
import functools
import math

import jax
import jax.numpy as jnp
from jax import lax
from jax.experimental import pallas as pl
from jax.experimental.pallas import tpu as pltpu
from jax.sharding import PartitionSpec as P

D = 1600
HEADS = 25
HEAD_DIM = 64
GROUPS = 13
WIDE = GROUPS * 128

epsilon = 1e-05
gelu_coeff = 0.7978845608028654
MESH = pl.DeviceIdType.MESH
f32, bf16 = jnp.float32, jnp.bfloat16


def place():
    me = lax.axis_index("ctx")
    return me, me // 4, (me // 2) % 2, me % 2


def greet(targets):
    barrier = pltpu.get_barrier_semaphore()
    count = 0
    for ok, t in targets:
        if ok is None:
            pl.semaphore_signal(barrier, inc=1, device_id={"ctx": t}, device_id_type=MESH)
            count = count + 1
        else:
            @pl.when(ok)
            def _(t=t):
                pl.semaphore_signal(barrier, inc=1, device_id={"ctx": t}, device_id_type=MESH)
            count = count + jnp.where(ok, 1, 0)
    pl.semaphore_wait(barrier, count)


def product(acc, a, b_ref):
    width = b_ref.shape[1]
    first = 0
    while first < width:
        last = width if width - first < 1024 else first + 512
        acc[:, first:last] = lax.dot_general(
            a, b_ref[:, first:last], (((1,), (0,)), ((), ())), preferred_element_type=jnp.float32)
        first = last


def rows_of(rows, fn, c, step=16):
    @pl.loop(0, rows // step)
    def _(i):
        fn(pl.ds(pl.multiple_of(c * rows + i * step, step), step))


def gather_kernel(Z, C, x_ref, out_ref, ssem, rsem, lsem):
    me, z, y, k = place()
    rows = x_ref.shape[0] // C
    right, left = jnp.minimum(me + 4, 4 * Z - 1), jnp.maximum(me - 4, 0)
    ypart, cpart = me + 2 - 4 * y, me + 1 - 2 * k
    has_r, has_l = z < Z - 1, z > 0
    greet([(has_r, right), (has_l, left), (None, ypart), (None, cpart)])
    local = pltpu.make_async_copy(x_ref, out_ref.at[me], lsem)
    local.start()
    where = (right, left, ypart, cpart)

    def desc(d, slot, c, src=None):
        part = out_ref.at[slot, pl.ds(c * rows, rows)]
        return pltpu.make_async_remote_copy(
            src_ref=part if src is None else src, dst_ref=part,
            send_sem=ssem.at[d, slot, c], recv_sem=rsem.at[d, slot, c],
            device_id={"ctx": where[d]}, device_id_type=MESH)

    for c in range(C):
        own = x_ref.at[pl.ds(c * rows, rows)]

        @pl.when(has_r)
        def _():
            desc(0, me, c, own).start()

        @pl.when(has_l)
        def _():
            desc(1, me, c, own).start()
        desc(2, me, c, own).start()
        desc(3, me, c, own).start()

    def slot_of(zz, yy, kk):
        return zz * 4 + yy * 2 + kk

    def from_y(zz, c):
        s = slot_of(zz, 1 - y, k)
        desc(2, s, c).wait_recv()
        desc(3, s, c).start()

    def from_y_at(t, c):
        @pl.when(z - t >= 0)
        def _():
            from_y(z - t, c)
        if t > 0:
            @pl.when(z + t <= Z - 1)
            def _():
                from_y(z + t, c)

    for t in range(Z - 1):
        for c in range(C):
            @pl.when(z - 1 - t >= 0)
            def _():
                s = slot_of(z - 1 - t, y, k)
                desc(0, s, c).wait_recv()

                @pl.when(has_r)
                def _():
                    desc(0, s, c).start()
                desc(2, s, c).start()
                desc(3, s, c).start()

            @pl.when(z + 1 + t <= Z - 1)
            def _():
                s = slot_of(z + 1 + t, y, k)
                desc(1, s, c).wait_recv()

                @pl.when(has_l)
                def _():
                    desc(1, s, c).start()
                desc(2, s, c).start()
                desc(3, s, c).start()
            from_y_at(t, c)
    for c in range(C):
        from_y_at(Z - 1, c)
    local.wait()
    for zz in range(Z):
        for c in range(C):
            for yy in range(2):
                desc(3, slot_of(zz, yy, 1 - k), c).wait_recv()
                desc(3, slot_of(zz, yy, k), c).wait_send()
            desc(2, slot_of(zz, y, k), c).wait_send()

            @pl.when((zz <= z) & has_r)
            def _():
                desc(0, slot_of(zz, y, k), c).wait_send()

            @pl.when((zz >= z) & has_l)
            def _():
                desc(1, slot_of(zz, y, k), c).wait_send()


def gather_ctx(x, Z, C, cid):
    n = 4 * Z
    dma = pltpu.SemaphoreType.DMA
    return pl.pallas_call(
        functools.partial(gather_kernel, Z, C),
        out_shape=jax.ShapeDtypeStruct((n,) + x.shape, x.dtype),
        in_specs=[pl.BlockSpec(memory_space=pltpu.VMEM)],
        out_specs=pl.BlockSpec(memory_space=pl.ANY),
        scratch_shapes=[dma((4, n, C)), dma((4, n, C)), dma],
        compiler_params=pltpu.CompilerParams(collective_id=cid, has_side_effects=True),
        name="gather_ctx",
    )(x)


def gather_cube_kernel(x_ref, out_ref, ssem, rsem, lsem):
    me, z, y, k = place()
    zl = z % 2
    rows = x_ref.shape[0] // 2
    zpart, ypart, cpart = me + 4 - 8 * zl, me + 2 - 4 * y, me + 1 - 2 * k
    greet([(None, zpart), (None, ypart), (None, cpart)])
    own = me % 8
    local = pltpu.make_async_copy(x_ref, out_ref.at[own], lsem)
    local.start()
    where = (zpart, ypart, cpart)

    def desc(d, slot, c, src=None):
        part = out_ref.at[slot, pl.ds(c * rows, rows)]
        return pltpu.make_async_remote_copy(
            src_ref=part if src is None else src, dst_ref=part,
            send_sem=ssem.at[d, slot, c], recv_sem=rsem.at[d, slot, c],
            device_id={"ctx": where[d]}, device_id_type=MESH)

    def slot_of(a, b, kk):
        return a * 4 + b * 2 + kk
    z_slot, y_slot, far = slot_of(1 - zl, y, k), slot_of(zl, 1 - y, k), slot_of(1 - zl, 1 - y, k)
    for c in (0, 1):
        half = x_ref.at[pl.ds(c * rows, rows)]
        desc(c, own, c, half).start()
        desc(1 - c, own, c, half).start()
    for c in (0, 1):
        desc(2, own, c, x_ref.at[pl.ds(c * rows, rows)]).start()
    desc(0, z_slot, 0).wait_recv()
    desc(1, z_slot, 0).start()
    desc(1, y_slot, 1).wait_recv()
    desc(0, y_slot, 1).start()
    desc(2, z_slot, 0).start()
    desc(2, y_slot, 1).start()
    desc(0, z_slot, 1).wait_recv()
    desc(2, z_slot, 1).start()
    desc(1, y_slot, 0).wait_recv()
    desc(2, y_slot, 0).start()
    desc(1, far, 0).wait_recv()
    desc(2, far, 0).start()
    desc(0, far, 1).wait_recv()
    desc(2, far, 1).start()
    local.wait()
    for a in range(2):
        for b in range(2):
            for c in range(2):
                desc(2, slot_of(a, b, 1 - k), c).wait_recv()
                desc(2, slot_of(a, b, k), c).wait_send()
    for c in (0, 1):
        desc(0, own, c).wait_send()
        desc(1, own, c).wait_send()
    desc(1, z_slot, 0).wait_send()
    desc(0, y_slot, 1).wait_send()


def gather_cube(x, cid):
    dma = pltpu.SemaphoreType.DMA
    return pl.pallas_call(
        gather_cube_kernel,
        out_shape=jax.ShapeDtypeStruct((8,) + x.shape, x.dtype),
        in_specs=[pl.BlockSpec(memory_space=pltpu.VMEM)],
        out_specs=pl.BlockSpec(memory_space=pl.ANY),
        scratch_shapes=[dma((3, 8, 2)), dma((3, 8, 2)), dma],
        compiler_params=pltpu.CompilerParams(collective_id=cid, has_side_effects=True),
        name="gather_cube",
    )(x)


def scatter_kernel(C, a_ref, b_ref, o_ref, acc, stage, rc, ry, rz, cs, cr, ys, yr, zs, zr):
    me, z, y, k = place()
    Z = 4
    R = a_ref.shape[1]
    rows = R // C
    f = jnp.float32
    right, left = jnp.minimum(me + 4, 4 * Z - 1), jnp.maximum(me - 4, 0)
    ypart, cpart = me + 2 - 4 * y, me + 1 - 2 * k
    has_r, has_l = z < Z - 1, z > 0
    greet([(has_r, right), (has_l, left), (None, ypart), (None, cpart)])

    def target(i):
        end = (z == 0) | (z == Z - 1)
        v = jnp.where(end, 3 - i, jnp.where(i == 0, 3, jnp.where(i == 1, 0, jnp.where(i == 2, 2, 1))))
        return jnp.where(z < 2, v, 3 - v)

    def cd(zz, far, c):
        ds = pl.ds(c * rows, rows)
        s = zz * 2 + far
        return pltpu.make_async_remote_copy(
            src_ref=stage.at[s, ds], dst_ref=rc.at[s, ds], send_sem=cs.at[s, c], recv_sem=cr.at[s, c],
            device_id={"ctx": cpart}, device_id_type=MESH)

    def yd(zz, c):
        ds = pl.ds(c * rows, rows)
        return pltpu.make_async_remote_copy(
            src_ref=rc.at[zz * 2 + 1, ds], dst_ref=ry.at[zz, ds], send_sem=ys.at[zz, c], recv_sem=yr.at[zz, c],
            device_id={"ctx": ypart}, device_id_type=MESH)

    def zd(d, zz, c, first=False):
        ds = pl.ds(c * rows, rows)
        return pltpu.make_async_remote_copy(
            src_ref=ry.at[zz, ds] if first else rz.at[d, zz, ds], dst_ref=rz.at[d, zz, ds],
            send_sem=zs.at[d, zz, c], recv_sem=zr.at[d, zz, c],
            device_id={"ctx": (right, left)[d]}, device_id_type=MESH)

    def slot(zz, far, kk):
        return zz * 4 + (y + far - 2 * y * far) * 2 + kk

    for far in (1, 0):
        @pl.loop(0, Z)
        def _(i):
            zz = target(i)
            product(acc, a_ref[slot(zz, far, 1 - k)], b_ref)
            for c in range(C):
                def move(ds):
                    stage[zz * 2 + far, ds, :] = acc[ds, :].astype(stage.dtype)
                rows_of(rows, move, c)
                cd(zz, far, c).start()
        if far:
            continue

    @pl.loop(0, Z)
    def _(i):
        zz = target(i)
        product(acc, a_ref[slot(zz, 1, k)], b_ref)
        for c in range(C):
            cd(zz, 1, c).wait_recv()

            def join(ds):
                s = zz * 2 + 1
                rc[s, ds, :] = (rc[s, ds, :].astype(f) + acc[ds, :]).astype(rc.dtype)
            rows_of(rows, join, c)
            yd(zz, c).start()

    @pl.loop(0, Z - 1)
    def _(i):
        zz = target(i)
        product(acc, a_ref[slot(zz, 0, k)], b_ref)
        for c in range(C):
            cd(zz, 0, c).wait_recv()
            yd(zz, c).wait_recv()

            def join(ds):
                ry[zz, ds, :] = (acc[ds, :] + rc[zz * 2, ds, :].astype(f) + ry[zz, ds, :].astype(f)).astype(ry.dtype)
            rows_of(rows, join, c)
            for d, here, starts in ((0, zz > z, z == 0), (1, zz < z, z == Z - 1)):
                @pl.when(here & starts)
                def _():
                    zd(d, zz, c, True).start()

                @pl.when(here & jnp.logical_not(starts))
                def _():
                    zd(d, zz, c).wait_recv()

                    def add(ds):
                        rz[d, zz, ds, :] = (rz[d, zz, ds, :].astype(f) + ry[zz, ds, :].astype(f)).astype(rz.dtype)
                    rows_of(rows, add, c)
                    zd(d, zz, c).start()

    product(acc, a_ref[slot(z, 0, k)], b_ref)
    for c in range(C):
        cd(z, 0, c).wait_recv()
        yd(z, c).wait_recv()

        def join(ds):
            o_ref[ds, :] = acc[ds, :] + rc[z * 2, ds, :].astype(f) + ry[z, ds, :].astype(f)
        rows_of(rows, join, c)
        for d, here in ((0, has_l), (1, has_r)):
            @pl.when(here)
            def _():
                zd(d, z, c).wait_recv()

                def add(ds):
                    o_ref[ds, :] += rz[d, z, ds, :].astype(f)
                rows_of(rows, add, c)
    for c in range(C):
        @pl.loop(0, Z)
        def _(zz):
            for far in (0, 1):
                cd(zz, far, c).wait_send()
            yd(zz, c).wait_send()

            @pl.when(zz > z)
            def _():
                zd(0, zz, c).wait_send()

            @pl.when(zz < z)
            def _():
                zd(1, zz, c).wait_send()


def scatter_ctx(a, b, C, cid):
    n, R, _ = a.shape
    N, Z = b.shape[1], 4
    dma = pltpu.SemaphoreType.DMA
    vm = pl.BlockSpec(memory_space=pltpu.VMEM)
    low = jnp.bfloat16
    return pl.pallas_call(
        functools.partial(scatter_kernel, C),
        out_shape=jax.ShapeDtypeStruct((R, N), jnp.float32),
        in_specs=[vm, vm],
        out_specs=vm,
        scratch_shapes=[
            pltpu.VMEM((R, N), jnp.float32), pltpu.VMEM((2 * Z, R, N), low), pltpu.VMEM((2 * Z, R, N), low), pltpu.VMEM((Z, R, N), low),
            pltpu.VMEM((2, Z, R, N), low), dma((2 * Z, C)), dma((2 * Z, C)), dma((Z, C)), dma((Z, C)), dma((2, Z, C)), dma((2, Z, C)),
        ],
        compiler_params=pltpu.CompilerParams(collective_id=cid, has_side_effects=True, vmem_limit_bytes=60 << 20),
        name="scatter_ctx",
    )(a, b)


def scatter_cube_kernel(a_ref, b_ref, o_ref, acc, stage, rc, rz, ry, cs, cr, zs, zr, ys, yr):
    me, z, y, k = place()
    zl = z % 2
    R = a_ref.shape[1]
    rows = R // 2
    f = jnp.float32
    zpart, ypart, cpart = me + 4 - 8 * zl, me + 2 - 4 * y, me + 1 - 2 * k
    greet([(None, zpart), (None, ypart), (None, cpart)])
    FAR, ZN, YN, OWN = range(4)

    def slot(i, kk):
        flip_z = jnp.where(i < 2, 1, 0)
        flip_y = jnp.where((i == 0) | (i == 2), 1, 0)
        return (zl + flip_z - 2 * zl * flip_z) * 4 + (y + flip_y - 2 * y * flip_y) * 2 + kk

    def cd(i):
        return pltpu.make_async_remote_copy(
            src_ref=stage.at[i], dst_ref=rc.at[i], send_sem=cs.at[i], recv_sem=cr.at[i],
            device_id={"ctx": cpart}, device_id_type=MESH)

    def link(over_z, i, c, dst):
        land, ss, rs = (rz, zs, zr) if over_z else (ry, ys, yr)
        return pltpu.make_async_remote_copy(
            src_ref=rc.at[i, pl.ds(c * rows, rows)], dst_ref=land.at[dst], send_sem=ss.at[dst], recv_sem=rs.at[dst],
            device_id={"ctx": zpart if over_z else ypart}, device_id_type=MESH)

    @pl.loop(0, 4)
    def _(i):
        product(acc, a_ref[slot(i, 1 - k)], b_ref)

        def move(ds):
            stage[i, ds, :] = acc[ds, :].astype(stage.dtype)
        rows_of(R, move, 0)
        cd(i).start()

    def chip_sum(i):
        product(acc, a_ref[slot(i, k)], b_ref)
        cd(i).wait_recv()

        def join(ds):
            rc[i, ds, :] = (rc[i, ds, :].astype(f) + acc[ds, :]).astype(rc.dtype)
        rows_of(R, join, 0)

    def pass_on(land, i, c):
        def add(ds):
            dst = pl.ds(pl.multiple_of(ds.start - c * rows, 16), 16)
            rc[i, ds, :] = (rc[i, ds, :].astype(f) + land[2, dst, :].astype(f)).astype(rc.dtype)
        rows_of(rows, add, c)

    chip_sum(FAR)
    link(True, FAR, 0, 2).start()
    link(False, FAR, 1, 2).start()
    chip_sum(ZN)
    link(True, ZN, 0, 0).start()
    chip_sum(YN)
    link(False, YN, 1, 1).start()
    link(True, FAR, 0, 2).wait_recv()
    pass_on(rz, YN, 0)
    link(False, YN, 0, 0).start()
    link(False, FAR, 1, 2).wait_recv()
    pass_on(ry, ZN, 1)
    link(True, ZN, 1, 1).start()
    product(acc, a_ref[slot(OWN, k)], b_ref)
    cd(OWN).wait_recv()

    def join(ds):
        o_ref[ds, :] = acc[ds, :] + rc[OWN, ds, :].astype(f)
    rows_of(R, join, 0)
    for over_z, c in ((True, 0), (False, 1), (False, 0), (True, 1)):
        link(over_z, OWN, c, c).wait_recv()
        land = rz if over_z else ry

        def add(ds):
            dst = pl.ds(pl.multiple_of(ds.start - c * rows, 16), 16)
            o_ref[ds, :] += land[c, dst, :].astype(f)
        rows_of(rows, add, c)
    for i in range(4):
        cd(i).wait_send()
    for over_z in (True, False):
        for dst in range(3):
            link(over_z, FAR, 0, dst).wait_send()


def scatter_cube(a, b, cid):
    n, R, _ = a.shape
    N = b.shape[1]
    dma = pltpu.SemaphoreType.DMA
    vm = pl.BlockSpec(memory_space=pltpu.VMEM)
    low = jnp.bfloat16
    return pl.pallas_call(
        scatter_cube_kernel,
        out_shape=jax.ShapeDtypeStruct((R, N), jnp.float32),
        in_specs=[vm, vm],
        out_specs=vm,
        scratch_shapes=[
            pltpu.VMEM((R, N), jnp.float32), pltpu.VMEM((4, R, N), low), pltpu.VMEM((4, R, N), low), pltpu.VMEM((3, R // 2, N), low),
            pltpu.VMEM((3, R // 2, N), low), dma((4,)), dma((4,)), dma((3,)), dma((3,)), dma((3,)), dma((3,)),
        ],
        compiler_params=pltpu.CompilerParams(collective_id=cid, has_side_effects=True, vmem_limit_bytes=60 << 20),
        name="scatter_cube",
    )(a, b)


def greet_all(n_x, n_c):
    barrier = pltpu.get_barrier_semaphore()
    me = lax.axis_index("fsdp") * n_c + lax.axis_index("ctx")
    n = n_x * n_c

    @pl.loop(1, n)
    def _(i):
        d = (me + i) % n
        pl.semaphore_signal(barrier, inc=1, device_id={"fsdp": d // n_c, "ctx": d % n_c}, device_id_type=MESH)
    pl.semaphore_wait(barrier, n - 1)


def spread_kernel(n_x, n_c, wt_ref, vec_ref, wh_ref, wout_ref, vall_ref, us, ur, os, orr, vs, vr, ls):
    x, ctx = lax.axis_index("fsdp"), lax.axis_index("ctx")
    n = n_x * n_c
    me = x * n_c + ctx
    U = wt_ref.shape[0]
    first_out = 3 * n // 4
    per = U * n // 4
    greet_all(n_x, n_c)

    def vec_copy(i, sending):
        d = (me + i) % n if sending else (me + n - i) % n
        slot = me if sending else d
        return pltpu.make_async_remote_copy(
            src_ref=vec_ref, dst_ref=vall_ref.at[slot], send_sem=vs.at[i], recv_sem=vr.at[slot],
            device_id={"fsdp": d // n_c, "ctx": d % n_c}, device_id_type=MESH)

    @pl.loop(1, n)
    def _(i):
        vec_copy(i, True).start()
    own_vec = pltpu.make_async_copy(vec_ref, vall_ref.at[me], ls)
    own_vec.start()

    def unit_target(u):
        g = U * me + u
        return (g % per) // 16, (g // per) * 16 + (g % per) % 16

    def unit_copy(u, to_x, j, slot):
        return pltpu.make_async_remote_copy(
            src_ref=wt_ref.at[u], dst_ref=wh_ref.at[slot], send_sem=us.at[u, to_x], recv_sem=ur.at[slot],
            device_id={"fsdp": to_x, "ctx": j}, device_id_type=MESH)

    def unit_local(u, slot):
        return pltpu.make_async_copy(wt_ref.at[u], wh_ref.at[slot], ur.at[slot])

    def out_copy(j, to_x, o):
        return pltpu.make_async_remote_copy(
            src_ref=wt_ref.at[:, :, pl.ds(pl.multiple_of(j * 128, 128), 128)], dst_ref=wout_ref.at[pl.ds(U * o, U)],
            send_sem=os.at[j, to_x], recv_sem=orr.at[o], device_id={"fsdp": to_x, "ctx": j}, device_id_type=MESH)

    def out_local(j, o):
        return pltpu.make_async_copy(
            wt_ref.at[:, :, pl.ds(pl.multiple_of(j * 128, 128), 128)], wout_ref.at[pl.ds(U * o, U)], orr.at[o])

    def sends(remote, local):
        @pl.when(me < first_out)
        def _():
            @pl.loop(0, U)
            def _(u):
                j, slot = unit_target(u)
                for to_x in range(n_x):
                    here = (x == to_x) & (ctx == j)

                    @pl.when(jnp.logical_not(here))
                    def _():
                        remote(unit_copy(u, to_x, j, slot))
                    if local is not None:
                        @pl.when(here)
                        def _():
                            local(unit_local(u, slot))

        @pl.when(me >= first_out)
        def _():
            @pl.loop(0, GROUPS)
            def _(j):
                for to_x in range(n_x):
                    here = (x == to_x) & (ctx == j)

                    @pl.when(jnp.logical_not(here))
                    def _():
                        remote(out_copy(j, to_x, me - first_out))
                    if local is not None:
                        @pl.when(here)
                        def _():
                            local(out_local(j, me - first_out))

    sends(lambda c: c.start(), lambda c: c.start())
    own_vec.wait()

    @pl.loop(1, n)
    def _(i):
        vec_copy(i, False).wait_recv()

    @pl.when(ctx < GROUPS)
    def _():
        @pl.loop(0, 48)
        def _(slot):
            e = ctx * 16 + slot % 16
            g = (slot // 16) * per + e
            owner = g // U

            @pl.when(e < per)
            def _():
                @pl.when(owner == me)
                def _():
                    unit_local(g % U, slot).wait()

                @pl.when(owner != me)
                def _():
                    unit_copy(g % U, 1 - x, ctx, slot).wait_recv()

        @pl.loop(0, n // 4)
        def _(o):
            @pl.when(o + first_out == me)
            def _():
                out_local(ctx, o).wait()

            @pl.when(o + first_out != me)
            def _():
                out_copy(ctx, 1 - x, o).wait_recv()

    @pl.loop(1, n)
    def _(i):
        vec_copy(i, True).wait_send()
    sends(lambda c: c.wait_send(), None)


def spread(wt, vec, n_x, n_c, cid):
    n = n_x * n_c
    U = wt.shape[0]
    dma = pltpu.SemaphoreType.DMA
    vm, hbm = pl.BlockSpec(memory_space=pltpu.VMEM), pl.BlockSpec(memory_space=pl.ANY)
    return pl.pallas_call(
        functools.partial(spread_kernel, n_x, n_c),
        out_shape=(
            jax.ShapeDtypeStruct((48, 8, WIDE), bf16),
            jax.ShapeDtypeStruct((U * n // 4, 8, 128), bf16),
            jax.ShapeDtypeStruct((n, 8, 128), f32),
        ),
        in_specs=[vm, vm],
        out_specs=(hbm, hbm, hbm),
        scratch_shapes=[dma((U, n_x)), dma((48,)), dma((GROUPS, n_x)), dma((n // 4,)), dma((n,)), dma((n,)), dma],
        compiler_params=pltpu.CompilerParams(collective_id=cid, has_side_effects=True),
        name="spread",
    )(wt, vec)


def collect_kernel(n_x, n_c, U, gh_ref, gout_ref, r_ref, us, ur, os, orr):
    x, ctx = lax.axis_index("fsdp"), lax.axis_index("ctx")
    n = n_x * n_c
    me = x * n_c + ctx
    first_out = 3 * n // 4
    per = U * n // 4
    greet_all(n_x, n_c)

    def unit_copy(from_x, slot, owner, u):
        return pltpu.make_async_remote_copy(
            src_ref=gh_ref.at[slot], dst_ref=r_ref.at[from_x, u], send_sem=us.at[slot], recv_sem=ur.at[from_x, u],
            device_id={"fsdp": owner // n_c, "ctx": owner % n_c}, device_id_type=MESH)

    def unit_local(slot, u):
        return pltpu.make_async_copy(gh_ref.at[slot], r_ref.at[x, u], ur.at[x, u])

    def out_copy(from_x, j, o):
        owner = first_out + o
        return pltpu.make_async_remote_copy(
            src_ref=gout_ref.at[pl.ds(U * o, U)], dst_ref=r_ref.at[from_x, :, :, pl.ds(pl.multiple_of(j * 128, 128), 128)],
            send_sem=os.at[o], recv_sem=orr.at[from_x, j],
            device_id={"fsdp": owner // n_c, "ctx": owner % n_c}, device_id_type=MESH)

    def out_local(j, o):
        return pltpu.make_async_copy(
            gout_ref.at[pl.ds(U * o, U)], r_ref.at[x, :, :, pl.ds(pl.multiple_of(j * 128, 128), 128)], orr.at[x, j])

    def sends(remote, local):
        @pl.when(ctx < GROUPS)
        def _():
            @pl.loop(0, 48)
            def _(slot):
                e = ctx * 16 + slot % 16
                g = (slot // 16) * per + e

                @pl.when((e < per) & (g // U != me))
                def _():
                    remote(unit_copy(x, slot, g // U, g % U))
                if local is not None:
                    @pl.when((e < per) & (g // U == me))
                    def _():
                        local(unit_local(slot, g % U))

            @pl.loop(0, n // 4)
            def _(o):
                @pl.when(o + first_out != me)
                def _():
                    remote(out_copy(x, ctx, o))
                if local is not None:
                    @pl.when(o + first_out == me)
                    def _():
                        local(out_local(ctx, o))

    sends(lambda c: c.start(), lambda c: c.start())

    @pl.when(me < first_out)
    def _():
        for from_x in range(n_x):
            @pl.loop(0, U)
            def _(u):
                g = U * me + u
                j, slot = (g % per) // 16, (g // per) * 16 + (g % per) % 16
                here = (x == from_x) & (ctx == j)

                @pl.when(here)
                def _():
                    unit_local(slot, u).wait()

                @pl.when(jnp.logical_not(here))
                def _():
                    unit_copy(from_x, slot, (me + 1) % n, u).wait_recv()

    @pl.when(me >= first_out)
    def _():
        for from_x in range(n_x):
            @pl.loop(0, GROUPS)
            def _(j):
                here = (x == from_x) & (ctx == j)

                @pl.when(here)
                def _():
                    out_local(j, me - first_out).wait()

                @pl.when(jnp.logical_not(here))
                def _():
                    out_copy(from_x, j, 0).wait_recv()
    sends(lambda c: c.wait_send(), None)


def collect(gh, gout, n_x, n_c, cid):
    n = n_x * n_c
    U = gout.shape[0] * 4 // n
    dma = pltpu.SemaphoreType.DMA
    hbm = pl.BlockSpec(memory_space=pl.ANY)
    return pl.pallas_call(
        functools.partial(collect_kernel, n_x, n_c, U),
        out_shape=jax.ShapeDtypeStruct((n_x, U, 8, WIDE), bf16),
        in_specs=[hbm, hbm],
        out_specs=hbm,
        scratch_shapes=[dma((48,)), dma((n_x, U)), dma((n // 4,)), dma((n_x, GROUPS))],
        compiler_params=pltpu.CompilerParams(collective_id=cid, has_side_effects=True),
        name="collect",
    )(gh, gout)


def reduce_kernel(n_x, n_c, p_ref, o_ref, land, ss, rs):
    n = n_x * n_c
    me = lax.axis_index("fsdp") * n_c + lax.axis_index("ctx")
    greet_all(n_x, n_c)

    def copy(i, sending):
        d = (me + i) % n if sending else (me + n - i) % n
        return pltpu.make_async_remote_copy(
            src_ref=p_ref.at[d], dst_ref=land.at[i], send_sem=ss.at[i], recv_sem=rs.at[i],
            device_id={"fsdp": d // n_c, "ctx": d % n_c}, device_id_type=MESH)

    @pl.loop(1, n)
    def _(i):
        copy(i, True).start()

    @pl.loop(1, n)
    def _(i):
        copy(i, False).wait_recv()
    o_ref[...] = lax.fori_loop(1, n, lambda i, s: s + land[i], p_ref[me])

    @pl.loop(1, n)
    def _(i):
        copy(i, True).wait_send()


def reduce_vectors(p, n_x, n_c, cid):
    n = n_x * n_c
    dma = pltpu.SemaphoreType.DMA
    vm = pl.BlockSpec(memory_space=pltpu.VMEM)
    return pl.pallas_call(
        functools.partial(reduce_kernel, n_x, n_c),
        out_shape=jax.ShapeDtypeStruct(p.shape[1:], f32),
        in_specs=[vm],
        out_specs=vm,
        scratch_shapes=[pltpu.VMEM(p.shape, f32), dma((n,)), dma((n,))],
        compiler_params=pltpu.CompilerParams(collective_id=cid, has_side_effects=True),
        name="reduce_vectors",
    )(p)


def dot(a, b, dims):
    return lax.dot_general(a, b, (dims, ((), ())), preferred_element_type=f32)

def attn_fwd_kernel(B, scale, q_ref, k_ref, v_ref, o_ref, lse_ref, qm, vt):
    S = q_ref.shape[0]
    lane = lax.broadcasted_iota(jnp.int32, (1, 128), 1)
    sub = lax.broadcasted_iota(jnp.int32, (128, 1), 0)
    nb = S // B

    @pl.loop(0, nb)
    def _(i):
        ds = pl.ds(pl.multiple_of(i * B, B), B)
        q = q_ref[ds, :].astype(f32) * scale
        v = v_ref[ds, :].astype(f32).T
        for h in range(2):
            qm[h, ds, :] = jnp.where(lane // 64 == h, q, 0.0).astype(bf16)
            vt[h, :, ds] = jnp.where(sub // 64 == h, v, 0.0).astype(bf16)

    row = lax.broadcasted_iota(jnp.int32, (B, B), 0)
    col = lax.broadcasted_iota(jnp.int32, (B, B), 1)

    @pl.loop(0, nb)
    def _(i):
        qs = pl.ds(pl.multiple_of(i * B, B), B)

        def block(j, carry, diag):
            m, l, acc = carry
            ks = pl.ds(pl.multiple_of(j * B, B), B)
            k = k_ref[ks, :]
            new_m, new_l, facs, parts = [], [], [], []
            for h in range(2):
                s = dot(k, qm[h, qs, :], ((1,), (1,)))
                if diag:
                    s = jnp.where(row <= col, s, -jnp.inf)
                mh = jnp.maximum(m[h], jnp.max(s, axis=0, keepdims=True))
                p = jnp.exp(s - mh)
                fac = jnp.exp(m[h] - mh)
                new_m.append(mh)
                new_l.append(l[h] * fac + jnp.sum(p, axis=0, keepdims=True))
                facs.append(fac)
                parts.append(dot(vt[h, :, ks], p.astype(bf16), ((1,), (0,))))
            acc = acc * jnp.where(sub // 64 == 0, facs[0], facs[1]) + (parts[0] + parts[1])
            return tuple(new_m), tuple(new_l), acc

        init = (
            (jnp.full((1, B), -1e30, f32),) * 2,
            (jnp.zeros((1, B), f32),) * 2,
            jnp.zeros((128, B), f32),
        )
        carry = lax.fori_loop(0, i, lambda j, c: block(j, c, False), init)
        m, l, acc = block(i, carry, True)
        acc = acc / jnp.where(sub // 64 == 0, l[0], l[1])
        o_ref[qs, :] = acc.T.astype(bf16)
        for h in range(2):
            lse_ref[pl.ds(h, 1), qs] = m[h] + jnp.log(l[h])

def attn_fwd(q, k, v, B=512, scale=0.125):
    S = q.shape[0]
    return pl.pallas_call(
        functools.partial(attn_fwd_kernel, B, scale),
        out_shape=(jax.ShapeDtypeStruct((S, 128), bf16), jax.ShapeDtypeStruct((2, S), f32)),
        in_specs=[pl.BlockSpec(memory_space=pltpu.VMEM)] * 3,
        out_specs=(pl.BlockSpec(memory_space=pltpu.VMEM),) * 2,
        scratch_shapes=[pltpu.VMEM((2, S, 128), bf16), pltpu.VMEM((2, 128, S), bf16)],
        compiler_params=pltpu.CompilerParams(vmem_limit_bytes=48 << 20),
        cost_estimate=pl.CostEstimate(flops=4 * S * S * 128, bytes_accessed=S * 1024, transcendentals=S * S),
        name="attn_fwd",
    )(q, k, v)

def attn_bwd_kernel(B, scale, q_ref, k_ref, v_ref, g_ref, o_ref, lse_ref, dq_ref, dk_ref, dv_ref, sums_ref, qm, gm, kt, delta, dqt):
    S = q_ref.shape[0]
    lane = lax.broadcasted_iota(jnp.int32, (1, 128), 1)
    sub = lax.broadcasted_iota(jnp.int32, (128, 1), 0)
    nb = S // B

    @pl.loop(0, nb)
    def _(i):
        ds = pl.ds(pl.multiple_of(i * B, B), B)
        q = q_ref[ds, :].astype(f32) * scale
        g = g_ref[ds, :].astype(f32)
        kk = (k_ref[ds, :].astype(f32) * scale).T
        go = (g * o_ref[ds, :].astype(f32)).T
        for h in range(2):
            qm[h, ds, :] = jnp.where(lane // 64 == h, q, 0.0).astype(bf16)
            gm[h, ds, :] = jnp.where(lane // 64 == h, g, 0.0).astype(bf16)
            kt[h, :, ds] = jnp.where(sub // 64 == h, kk, 0.0).astype(bf16)
            delta[pl.ds(h, 1), ds] = jnp.sum(jnp.where(sub // 64 == h, go, 0.0), axis=0, keepdims=True)
        dqt[:, ds] = jnp.zeros((128, B), f32)

    row = lax.broadcasted_iota(jnp.int32, (B, B), 0)
    col = lax.broadcasted_iota(jnp.int32, (B, B), 1)

    def over_keys(j, sum_v):
        ks = pl.ds(pl.multiple_of(j * B, B), B)
        k, v = k_ref[ks, :], v_ref[ks, :]

        def block(i, carry, diag):
            dk, dv = carry
            qs = pl.ds(pl.multiple_of(i * B, B), B)
            upd = None
            for h in range(2):
                q, g = qm[h, qs, :], gm[h, qs, :]
                s = dot(k, q, ((1,), (1,)))
                if diag:
                    s = jnp.where(row <= col, s, -jnp.inf)
                p = jnp.exp(s - lse_ref[pl.ds(h, 1), qs])
                dp = dot(v, g, ((1,), (1,)))
                ds_ = (p * (dp - delta[pl.ds(h, 1), qs])).astype(bf16)
                dv = dv + dot(p.astype(bf16), g, ((1,), (0,)))
                dk = dk + dot(ds_, q, ((1,), (0,)))
                t = dot(kt[h, :, ks], ds_, ((1,), (0,)))
                upd = t if upd is None else upd + t
            dqt[:, qs] += upd
            return dk, dv

        zero = jnp.zeros((B, 128), f32)
        carry = block(j, (zero, zero), True)
        dk, dv = lax.fori_loop(j + 1, nb, lambda i, c: block(i, c, False), carry)
        dk_ref[ks, :] = dk.astype(bf16)
        dv_ref[ks, :] = dv.astype(bf16)
        return sum_v + jnp.sum(dv, axis=0, keepdims=True)

    sum_v = lax.fori_loop(0, nb, over_keys, jnp.zeros((1, 128), f32))

    def finish(i, sum_q):
        ds = pl.ds(pl.multiple_of(i * B, B), B)
        dq = dqt[:, ds].T
        dq_ref[ds, :] = dq.astype(bf16)
        return sum_q + jnp.sum(dq, axis=0, keepdims=True)

    sum_q = lax.fori_loop(0, nb, finish, jnp.zeros((1, 128), f32))
    sums_ref[pl.ds(0, 1), :] = sum_q
    sums_ref[pl.ds(1, 1), :] = sum_v

def attn_bwd(q, k, v, g, o, lse, B=512, scale=0.125):
    S = q.shape[0]
    vm = pl.BlockSpec(memory_space=pltpu.VMEM)
    return pl.pallas_call(
        functools.partial(attn_bwd_kernel, B, scale),
        out_shape=(jax.ShapeDtypeStruct((S, 128), bf16),) * 3 + (jax.ShapeDtypeStruct((2, 128), f32),),
        in_specs=[vm] * 6,
        out_specs=(vm,) * 4,
        scratch_shapes=[pltpu.VMEM((2, S, 128), bf16), pltpu.VMEM((2, S, 128), bf16), pltpu.VMEM((2, 128, S), bf16), pltpu.VMEM((2, S), f32), pltpu.VMEM((128, S), f32)],
        compiler_params=pltpu.CompilerParams(vmem_limit_bytes=56 << 20),
        cost_estimate=pl.CostEstimate(flops=10 * S * S * 128, bytes_accessed=S * 2560, transcendentals=S * S),
        name="attn_bwd",
    )(q, k, v, g, o, lse)


def layer_norm(values, gain_vec, shift_vec):
    center = values - jnp.mean(values, axis=-1, keepdims=True)
    spread_of = jnp.mean(center * center, axis=-1, keepdims=True)
    return center * lax.rsqrt(spread_of + epsilon) * gain_vec + shift_vec


def gelu_tanh(values):
    return 0.5 * values * (1.0 + jnp.tanh(gelu_coeff * (values + 0.044715 * values * values * values)))


def per_device(block_input, attn_weight, fc_weight, down_weight, vectors, cotangent):
    n_x, n_c = lax.axis_size("fsdp"), lax.axis_size("ctx")
    n = n_x * n_c
    x, ctx = lax.axis_index("fsdp"), lax.axis_index("ctx")
    me = x * n_c + ctx
    both = ("fsdp", "ctx")
    inputs, grad_output = block_input[0], cotangent[0]
    rows = inputs.shape[0]
    tokens = rows * n_c
    cols = attn_weight.shape[1]
    owned = vectors.shape[0]
    fast = n_x == 2 and n_c == 16 and cols % 8 == 0 and rows == 128
    ids = iter(range(1, 100))
    half = ctx // 8
    other_x = [(i, (i + 1) % n_x) for i in range(n_x)]
    other_half = [(i, (i + 8) % n_c) for i in range(n_c)]

    def swap_x(part):
        return lax.ppermute(part, "fsdp", other_x)

    def swap_half(part):
        return lax.ppermute(part, "ctx", other_half)

    attn_rows = attn_weight.T
    if fast:
        own_rows = jnp.concatenate([fc_weight.T, down_weight.T])
        half_rows = swap_half(own_rows)
        x_rows = swap_x(own_rows)
        both_rows = swap_x(half_rows)
        four = (own_rows, half_rows, x_rows, both_rows)
        fc_rows = jnp.concatenate([part[:cols] for part in four])
        down_rows = jnp.concatenate([part[cols:] for part in four])
        owners = [me, x * n_c + (ctx + 8) % n_c, (1 - x) * n_c + ctx, (1 - x) * n_c + (ctx + 8) % n_c]
    else:
        fc_rows = lax.all_gather(fc_weight.T, "fsdp", axis=0, tiled=True)
        down_rows = lax.all_gather(down_weight.T, "fsdp", axis=0, tiled=True)
        owners = [i * n_c + ctx for i in range(n_x)]

    def gather(part):
        if fast:
            return gather_ctx(part, n_c // 4, 2, next(ids)).reshape(tokens, -1)
        return lax.all_gather(part, "ctx", axis=0, tiled=True)

    def gather_near(part):
        if fast:
            return gather_cube(part, next(ids)).reshape(8 * rows, -1)
        return lax.all_gather(part, "ctx", axis=0, tiled=True)

    def scatter(left, right):
        if fast:
            return scatter_ctx(left.reshape(n_c, rows, -1), right, 2, next(ids))
        return lax.psum_scatter(dot(left, right, ((1,), (0,))), "ctx", scatter_dimension=0, tiled=True)

    def scatter_near(left, right):
        if fast:
            return scatter_cube(left.reshape(8, rows, -1), right, next(ids))
        return lax.psum_scatter(dot(left, right, ((1,), (0,))), "ctx", scatter_dimension=0, tiled=True)

    if fast:
        wt = jnp.pad(attn_rows, ((0, 0), (0, WIDE - D))).reshape(cols // 8, 8, WIDE)
        vec = jnp.pad(vectors.astype(f32), (0, 1024 - owned)).reshape(8, 128)
        head_units, out_units, vec_all = spread(wt, vec, n_x, n_c, next(ids))
        vec_full = vec_all.reshape(n, 1024)[:, :owned].reshape(-1)
        head_rows = head_units.reshape(3, 128, WIDE)[:, :, :D]
        live = ctx * 128 + jnp.arange(128, dtype=jnp.int32) < D
        head_rows = jnp.where(live[None, :, None], head_rows, 0).reshape(384, D)
        out_rows = jnp.where(live[None, :], out_units.reshape(D, 128), 0)
    else:
        full = lax.all_gather(attn_rows, both, axis=0, tiled=True)
        vec_full = lax.all_gather(vectors, both, axis=0, tiled=True).astype(f32)
        extra = n_c * 128 - D
        head_rows = jnp.pad(full[: 3 * D].reshape(3, D, D), ((0, 0), (0, extra), (0, 0)))
        head_rows = lax.dynamic_slice_in_dim(head_rows, ctx * 128, 128, 1).reshape(384, D)
        out_rows = lax.dynamic_slice_in_dim(jnp.pad(full[3 * D :], ((0, 0), (0, extra))), ctx * 128, 128, 1)

    def vec_at(block):
        return vec_full[block * D : (block + 1) * D]

    def heads_of(block):
        return lax.dynamic_slice_in_dim(jnp.pad(vec_at(block), (0, n_c * 128 - D)), ctx * 128, 128, 0)

    gain_one, shift_one, bias_out = vec_at(0), vec_at(1), vec_at(4)
    gain_two, shift_two, bias_down = vec_at(5), vec_at(6), vec_at(7)
    bias_heads = jnp.concatenate([heads_of(2), jnp.zeros((128,), f32), heads_of(3)])
    up_first = [8 * D + cols * owner for owner in owners]
    bias_up = jnp.concatenate([lax.dynamic_slice_in_dim(vec_full, first, cols, 0) for first in up_first])
    if fast:
        out_rows = jnp.concatenate([out_rows, swap_half(out_rows)], axis=1)
    out_back = out_rows.T

    normed_one, pull_one = jax.vjp(layer_norm, inputs, gain_one, shift_one)
    normed_one_all = gather(normed_one.astype(bf16))
    grad_low = grad_output.astype(bf16)
    normed_one_all, grad_low = lax.optimization_barrier((normed_one_all, grad_low))
    groups = [list(range(8)), list(range(8, 16))] if fast else None
    grad_low_all = lax.all_gather(grad_low, "ctx", axis=0, tiled=True, axis_index_groups=groups)
    qkv = (dot(normed_one_all, head_rows, ((1,), (1,))) + bias_heads).astype(bf16)
    queries, keys, values = qkv[:, :128], qkv[:, 128:256], qkv[:, 256:]
    mixed, log_total = attn_fwd(queries, keys, values, min(1024, tokens))
    mixed_near = mixed
    if fast:
        mixed_halves = mixed.reshape(2, tokens // 2, 128)
        got = swap_half(lax.dynamic_index_in_dim(mixed_halves, 1 - half, 0, False))
        mixed_near = jnp.concatenate([lax.dynamic_index_in_dim(mixed_halves, half, 0, False), got], axis=1)
    middle = inputs + scatter_near(mixed_near, out_back) + bias_out

    normed_two, pull_two = jax.vjp(layer_norm, middle, gain_two, shift_two)
    normed_two_all = gather_near(normed_two.astype(bf16))
    pre_act = dot(normed_two_all, fc_rows, ((1,), (1,))) + bias_up
    activated, pull_gelu = jax.vjp(gelu_tanh, pre_act)
    act_low = activated.astype(bf16)
    d_act = dot(grad_low_all, down_rows, ((1,), (1,)))
    d_pre = pull_gelu(d_act)[0]
    d_pre_low = d_pre.astype(bf16)
    d_normed_two = scatter_near(d_pre_low, fc_rows)
    d_normed_two, act_later = lax.optimization_barrier((d_normed_two, act_low))

    def weight_shard(left, right):
        part = dot(left, right, ((0,), (0,)))
        if fast:
            part = part[: 2 * cols] + swap_x(part[2 * cols :].astype(bf16)).astype(f32)
            return (part[:cols] + swap_half(part[cols:].astype(bf16)).astype(f32)).T
        return lax.psum_scatter(part, "fsdp", scatter_dimension=0, tiled=True).T

    down_shard = weight_shard(act_low, grad_low_all)
    fc_shard = weight_shard(d_pre_low, normed_two_all)

    d_middle_norm, grad_gain_two, grad_shift_two = pull_two(d_normed_two)
    d_middle = grad_output + d_middle_norm
    d_middle_all = gather_near(d_middle.astype(bf16))
    d_mixed = dot(d_middle_all, out_rows, ((1,), (0,))).astype(bf16)
    out_grads = dot(d_middle_all, mixed_near, ((0,), (0,)))
    if fast:
        got = swap_half(d_mixed[:, 128:])
        d_mixed = d_mixed[:, :128]
        d_mixed = jnp.concatenate([jnp.where(half == 0, d_mixed, got), jnp.where(half == 0, got, d_mixed)])
        out_grads = out_grads[:, :128] + swap_half(out_grads[:, 128:].astype(bf16)).astype(f32)
    block_output = middle + scatter_near(act_later, down_rows) + bias_down
    d_queries, d_keys, d_values, sums = attn_bwd(queries, keys, values, d_mixed, mixed, log_total, min(512, tokens))
    d_qkv = jnp.concatenate([d_queries, d_keys, d_values], axis=1)
    d_normed_one = scatter(d_qkv, head_rows)
    d_input_norm, grad_gain_one, grad_shift_one = pull_one(d_normed_one)
    input_grad = d_middle + d_input_norm
    head_grads = dot(d_qkv, normed_one_all, ((0,), (0,)))
    if fast:
        gh = jnp.pad(head_grads.astype(bf16), ((0, 0), (0, WIDE - D))).reshape(48, 8, WIDE)
        got = collect(gh, out_grads.astype(bf16).reshape(D // 8, 8, 128), n_x, n_c, next(ids))
        attn_shard = (got[0].astype(f32) + got[1].astype(f32)).reshape(cols, WIDE)[:, :D].T
    else:
        room = jnp.zeros((3, n_c * 128, D), f32)
        room = lax.dynamic_update_slice_in_dim(room, head_grads.reshape(3, 128, D), ctx * 128, 1)[:, :D].reshape(3 * D, D)
        room_out = lax.dynamic_update_slice_in_dim(jnp.zeros((D, n_c * 128), f32), out_grads, ctx * 128, 1)[:, :D]
        attn_shard = lax.psum_scatter(jnp.concatenate([room, room_out]), both, scatter_dimension=0, tiled=True).T

    def placed(part):
        return lax.dynamic_update_slice_in_dim(jnp.zeros((n_c * 128,), f32), part, ctx * 128, 0)[:D]

    d_pre_sum = jnp.sum(d_pre, axis=0)
    up_grads = jnp.zeros((4 * D,), f32)
    for i, first in enumerate(up_first):
        up_grads = lax.dynamic_update_slice_in_dim(up_grads, d_pre_sum[i * cols : (i + 1) * cols], first - 8 * D, 0)
    grad_vectors = jnp.concatenate(
        [
            grad_gain_one,
            grad_shift_one,
            placed(sums[0]),
            placed(sums[1]),
            jnp.sum(d_middle, axis=0),
            grad_gain_two,
            grad_shift_two,
            jnp.sum(grad_output, axis=0),
            up_grads,
        ]
    )
    if fast:
        parts = jnp.pad(grad_vectors.reshape(n, owned), ((0, 0), (0, 1024 - owned))).reshape(n, 8, 128)
        vector_shard = reduce_vectors(parts, n_x, n_c, next(ids)).reshape(-1)[:owned]
    else:
        vector_shard = lax.psum_scatter(grad_vectors, both, scatter_dimension=0, tiled=True)
    return (block_output[None], input_grad[None], attn_shard, fc_shard, down_shard, vector_shard)


def solution(mesh):
    tokens_spec = P("fsdp", "ctx", None)
    cols_spec = P(None, ("fsdp", "ctx"))
    vec_spec = P(("fsdp", "ctx"))
    return jax.shard_map(
        per_device,
        mesh=mesh,
        in_specs=(tokens_spec, cols_spec, cols_spec, cols_spec, vec_spec, tokens_spec),
        out_specs=(tokens_spec, tokens_spec, cols_spec, cols_spec, cols_spec, vec_spec),
        check_vma=False,
    )
```

time: 1770 us -> 675 us (0.38)
  waiting for transfers between devices: 1220 us -> 111 us
  Pallas kernels: 0 us -> 392 us
  starting transfers between devices: 199 us -> 24.4 us
  matrix products: 144 us -> 48.8 us
  local copies, waits for them, and re-layouts: 115 us -> 37.2 us
  blocking collectives: 40.1 us -> 0 us
    all_gather x9 -> x1, waiting for transfers between devices: 865 us -> 0.01 us  [per_device(): lax.all_gather(grad_low, 'ctx', axis=0, tiled=True, axis_index_groups=gro...]
    pallas_call x0 -> x12, Pallas kernels: none -> 392 us  [the longest x3 87.5 us: scatter_cube(): pl.pallas_call(scatter_cube_kernel, out_shape=jax.ShapeDtypeStruct((R, N)...]
    ppermute x80 -> x11, waiting for transfers between devices: 260 us -> 111 us  [the longest x7 107 us: swap_half(): return lax.ppermute(part, 'ctx', other_half)]
    ppermute x80 -> x11, starting transfers between devices: 172 us -> 24.4 us  [the longest x7 19.3 us: swap_half(): return lax.ppermute(part, 'ctx', other_half)]
    dot_general x21 -> x8, matrix products: 144 us -> 48.8 us  [dot(): return lax.dot_general(a, b, (dims, ((), ())), preferred_element_type=f32)]
    all_to_all x3 -> x0, waiting for transfers between devices: 63.8 us -> none  [the longest x1 32.8 us: per_device(): lax.all_to_all(attn_right, ('fsdp', 'ctx'), split_axis=1, concat_axis=0,...]
    while x80 -> x0, local copies, waits for them, and re-layouts: 50.4 us -> none
    unnamed x1 -> x0, blocking collectives: 40.1 us -> none
  transfers between devices with their start and end apart: 93 -> 12, of which waited for: 60 -> 5; matrix products, arithmetic and copies ran while one was open for 11% -> 13% of each run, Pallas kernels for 0% -> 50%
where the time goes in v1:
time: 675 us; the launch traced here: 668 us
  Pallas kernels  392 us (58%)
  waiting for transfers between devices  111 us (16%)
  matrix products  48.8 us (7%)
  other arithmetic  39.1 us (6%)
  local copies, waits for them, and re-layouts  37.2 us (6%)
  starting transfers between devices  24.4 us (4%)
  between operations  15 us (2%)
    ppermute x7, waiting for transfers between devices, swap_half(): return lax.ppermute(part, 'ctx', other_half)  107 us
    pallas_call x3, Pallas kernels, scatter_cube(): pl.pallas_call(scatter_cube_kernel, out_shape=jax.ShapeDtypeStruct((R, N)...  87.5 us
    pallas_call x1, Pallas kernels, collect(): pl.pallas_call(functools.partial(collect_kernel, n_x, n_c, U), out_shape=...  76.7 us
    pallas_call x1, Pallas kernels, gather_ctx(): pl.pallas_call(functools.partial(gather_kernel, Z, C), out_shape=jax.Shap...  59.7 us
    dot_general x8, matrix products, dot(): return lax.dot_general(a, b, (dims, ((), ())), preferred_element_type=f32)  48.8 us
    pallas_call x1, Pallas kernels, scatter_ctx(): pl.pallas_call(functools.partial(scatter_kernel, C), out_shape=jax.ShapeD...  46.6 us
    pallas_call x2, Pallas kernels, gather_cube(): pl.pallas_call(gather_cube_kernel, out_shape=jax.ShapeDtypeStruct((8,) +...  45.2 us
    pallas_call x1, Pallas kernels, spread(): pl.pallas_call(functools.partial(spread_kernel, n_x, n_c), out_shape=(jax...  35.3 us
  transfers between devices with their start and end apart: 12, of which 5 were waited for; matrix products, arithmetic and copies ran while one was open for 13% of the time, Pallas kernels for 50%

profile of v1, /device:TPU:31, one launch (start us, length us, event | category | flops | bytes accessed | tf_op | source)
XLA Modules:
  0.0 668.0 jit_solution(18353540807072470489)
XLA Ops:
  10.6 35.3 %spread.1 = (bf16[48,8,1664]{2,1,0:T(8,128)(2,1)}, bf16[200,8,128]{2,1,0:T(8,128)(2,1)}, f32[32,8,128]{2,1,0:T(8,128)}) custom-call(bf16[25,8,1664]{2,1,0:T(8,128)(2,1)} %pad_bitcast_fusion.1.wt_ref, f32[8,128]{1,0:T(8,128)} %bitcast_convert_fusion.1.vec_ref), custom_call_target="tpu_custom_call" | custom-call | tf_op jit(solution)/shard_map/spread/pallas_call | solution.py:609
  47.3 13.9 %collective-permute-start.1 = (bf16[1600,128]{0,1:T(8,128)(2,1)S(1)}, bf16[1600,128]{0,1:T(8,128)(2,1)}, u32[]{:S(2)}, u32[]{:S(2)}) collective-permute-start(bf16[1600,128]{0,1:T(8,128)(2,1)S(1)} %broadcast_select_fusion), channel_id=1, source_target_pairs={{0,8},{1,9},{2,10},{3,11},{4,12},{5,13},{6,14},{7,15},{8,0},{9,1},... | collective-permute-start | bytes 1228808 | tf_op jit(solution)/shard_map/ppermute | solution.py:949
  64.4 59.7 %gather_ctx.1 = bf16[16,128,1600]{2,1,0:T(8,128)(2,1)} custom-call(bf16[128,1600]{1,0:T(8,128)(2,1)} %add_convert_fusion.2.x_ref), custom_call_target="tpu_custom_call" | custom-call | tf_op jit(solution)/shard_map/gather_ctx/pallas_call | solution.py:153
  126.7 6.8 %add_convert_fusion = bf16[2048,384]{1,0:T(8,128)(2,1)S(1)} fusion(bf16[2048,1600]{1,0:T(8,128)(2,1)} %bitcast.92, bf16[384,1600]{1,0:T(8,128)(2,1)S(1)} %bitcast.94, f32[384]{0:T(512)S(1)} %pad_maximum_fusion.8), kind=kOutput, calls=%fused_computation.10 | convolution fusion | flops 2518155264 | bytes 9356800 | tf_op jit(solution)/shard_map/dot_general | solution.py:770
  133.8 8.7 %attn_fwd.1 = (bf16[2048,128]{1,0:T(8,128)(2,1)S(1)}, f32[2,2048]{1,0:T(2,128)S(1)}) custom-call(bf16[2048,128]{1,0:T(8,128)(2,1)S(1)} %get-tuple-element.62.q_ref, bf16[2048,128]{1,0:T(8,128)(2,1)S(1)} %get-tuple-element.61.k_ref, bf16[2048,128]{1,0:T(8,128)(2,1)S(1)} %get-tuple-element.60.v_ref), custom_call_target="tpu_custom_call" | custom-call | flops 2147483648 | bytes 2097152 | tf_op jit(solution)/shard_map/attn_fwd/pallas_call | solution.py:827
  148.0 38.3 %collective-permute-done = bf16[1024,128]{1,0:T(8,128)(2,1)} collective-permute-done((bf16[1024,128]{1,0:T(8,128)(2,1)S(1)}, bf16[1024,128]{1,0:T(8,128)(2,1)}, u32[]{:S(2)}, u32[]{:S(2)}) %collective-permute-start) | collective-permute-done | bytes 262176 | tf_op jit(solution)/shard_map/ppermute | solution.py:949
  190.0 40.1 %scatter_cube.3 = f32[128,1600]{1,0:T(8,128)} custom-call(bf16[8,128,256]{2,1,0:T(8,128)(2,1)} %pad_maximum_fusion.5.a_ref, bf16[256,1600]{1,0:T(8,128)(2,1)} %fusion.9.b_ref), custom_call_target="tpu_custom_call" | custom-call | tf_op jit(solution)/shard_map/scatter_cube/pallas_call | solution.py:462
  233.3 21.9 %gather_cube.2 = bf16[8,128,1600]{2,1,0:T(8,128)(2,1)} custom-call(bf16[128,1600]{1,0:T(8,128)(2,1)} %add_convert_fusion.1.x_ref), custom_call_target="tpu_custom_call" | custom-call | tf_op jit(solution)/shard_map/gather_cube/pallas_call | solution.py:220
  263.9 7.7 %pad_maximum_fusion = (bf16[800,1600]{1,0:T(8,128)(2,1)}, bf16[800,1600]{1,0:T(8,128)(2,1)}) fusion(bf16[200,1600]{1,0:T(8,128)(2,1)S(1)} %get-tuple-element.68, bf16[200,1600]{1,0:T(8,128)(2,1)S(1)} %get-tuple-element.66, bf16[200,1600]{1,0:T(8,128)(2,1)S(1)} %get-tuple-element.64, bf16[200,1600]{1,0:T(8,128)(2,1)S(1)} %bitcast.104, ...), kind=kLoop, calls=%fused_computation.16 | loop fusion | flops 20480000 | bytes 10240000 | tf_op jit(solution)/shard_map/concatenate | solution.py:958
  271.5 6.9 %multiply_convert_fusion = (bf16[1024,800]{0,1:T(8,128)(2,1)}, f32[1024,800]{0,1:T(8,128)}) fusion(f32[800]{0:T(1024)S(1)} %pad_maximum_fusion.7, bf16[1024,1600]{1,0:T(8,128)(2,1)S(1)} %bitcast.97, bf16[200,1600]{1,0:T(8,128)(2,1)S(1)} %get-tuple-element.68, bf16[200,1600]{1,0:T(8,128)(2,1)S(1)} %get-tuple-element.66, ...), kind=kOutput, calls=%fused_computation.9 | convolution fusion | flops 2639872000 | bytes 10755200 | tf_op jit(solution)/shard_map/dot_general | solution.py:770
  278.4 9.3 %fusion.26 = (f32[800]{0:T(1024)S(1)}, bf16[1024,800]{0,1:T(8,128)(2,1)}) fusion(bf16[1024,1600]{1,0:T(8,128)(2,1)} %all-gather.2.cloned.1.call-done, bf16[200,1600]{1,0:T(8,128)(2,1)} %copy-done.21, bf16[200,1600]{1,0:T(8,128)(2,1)} %copy-done.20, bf16[200,1600]{1,0:T(8,128)(2,1)S(1)} %get-tuple-element.63, bf16[200,1600]{1,0:T(8,128)(2,1)S(1)} %bitcast.108, ...), kind=kOutput, calls=%fused_computation.100 | convolution fusion | flops 2652978432 | bytes 10758400 | tf_op jit(solution)/shard_map/dot_general | solution.py:770
  291.6 6.7 %fusion.33 = f32[800,1600]{1,0:T(8,128)} fusion(bf16[1024,800]{0,1:T(8,128)(2,1)S(1)} %copy-done.25, bf16[1024,1600]{1,0:T(8,128)(2,1)} %bitcast.96), kind=kOutput, calls=%fused_computation.107 | convolution fusion | flops 2621440000 | bytes 10035200 | tf_op jit(solution)/shard_map/dot_general | solution.py:770
  298.3 25.1 %scatter_cube.4 = f32[128,1600]{1,0:T(8,128)} custom-call(bf16[8,128,800]{2,1,0:T(8,128)(2,1)} %bitcast.90, bf16[800,1600]{1,0:T(8,128)(2,1)} %get-tuple-element.91.b_ref), custom_call_target="tpu_custom_call" | custom-call | tf_op jit(solution)/shard_map/scatter_cube/pallas_call | solution.py:462
  330.5 22.3 %scatter_cube.5 = f32[128,1600]{1,0:T(8,128)} custom-call(bf16[8,128,800]{2,1,0:T(8,128)(2,1)} %bitcast.91, bf16[800,1600]{1,0:T(8,128)(2,1)} %get-tuple-element.92.b_ref), custom_call_target="tpu_custom_call" | custom-call | tf_op jit(solution)/shard_map/scatter_cube/pallas_call | solution.py:462
  356.6 5.6 fusion.34
  367.1 23.3 %gather_cube.3 = bf16[8,128,1600]{2,1,0:T(8,128)(2,1)} custom-call(bf16[128,1600]{1,0:T(8,128)(2,1)} %convert_element_type.82.x_ref), custom_call_target="tpu_custom_call" | custom-call | tf_op jit(solution)/shard_map/gather_cube/pallas_call | solution.py:220
  400.3 17.4 %collective-permute-done.5 = bf16[1024,128]{1,0:T(8,128)(2,1)S(1)} collective-permute-done((bf16[1024,128]{1,0:T(8,128)(2,1)S(1)}, bf16[1024,128]{1,0:T(8,128)(2,1)S(1)}, u32[]{:S(2)}, u32[]{:S(2)}) %collective-permute-start.5) | collective-permute-done | bytes 262176 | tf_op jit(solution)/shard_map/ppermute | solution.py:949
  418.5 19.4 %attn_bwd.1 = (bf16[2048,128]{1,0:T(8,128)(2,1)}, bf16[2048,128]{1,0:T(8,128)(2,1)}, bf16[2048,128]{1,0:T(8,128)(2,1)}, f32[2,128]{1,0:T(2,128)}) custom-call(bf16[2048,128]{1,0:T(8,128)(2,1)} %copy-done.3, bf16[2048,128]{1,0:T(8,128)(2,1)} %copy-done.2, bf16[2048,128]{1,0:T(8,128)(2,1)} %copy-done.1, bf16[2048,128]{1,0:T(8,128)(2,1)} %pad_maximum_fusion.6.g_ref, ...), custom_call_target="tpu_custom_call" | custom-call | flops 5368709120 | bytes 5242880 | tf_op jit(solution)/shard_map/attn_bwd/pallas_call | solution.py:906
  441.4 8.2 %convolution_convert_fusion = bf16[384,1600]{0,1:T(8,128)(2,1)} fusion(bf16[2048,384]{1,0:T(8,128)(2,1)S(1)} %constant_dynamic-update-slice_fusion, bf16[2048,1600]{1,0:T(8,128)(2,1)} %bitcast.93), kind=kOutput, calls=%fused_computation.11 | convolution fusion | flops 2517196800 | bytes 9355264 | tf_op jit(solution)/shard_map/dot_general | solution.py:770
  449.7 46.6 %scatter_ctx.1 = f32[128,1600]{1,0:T(8,128)} custom-call(bf16[16,128,384]{2,1,0:T(8,128)(2,1)} %bitcast.102, bf16[384,1600]{1,0:T(8,128)(2,1)} %bitcast.95), custom_call_target="tpu_custom_call" | custom-call | tf_op jit(solution)/shard_map/scatter_ctx/pallas_call | solution.py:359
  501.8 12.9 %reduce_vectors.1 = f32[8,128]{1,0:T(8,128)} custom-call(f32[32,8,128]{2,1,0:T(8,128)} %bitcast.113), custom_call_target="tpu_custom_call" | custom-call | tf_op jit(solution)/shard_map/reduce_vectors/pallas_call | solution.py:758
  520.2 76.7 %collect.1 = bf16[2,25,8,1664]{3,2,1,0:T(8,128)(2,1)} custom-call(bf16[48,8,1664]{2,1,0:T(8,128)(2,1)} %pad_bitcast_fusion.gh_ref, bf16[200,8,128]{2,1,0:T(8,128)(2,1)} %fusion.14.gout_ref), custom_call_target="tpu_custom_call" | custom-call | tf_op jit(solution)/shard_map/collect/pallas_call | solution.py:718
  606.3 38.5 %collective-permute-done.8 = bf16[200,1600]{1,0:T(8,128)(2,1)S(1)} collective-permute-done((bf16[200,1600]{1,0:T(8,128)(2,1)S(1)}, bf16[200,1600]{1,0:T(8,128)(2,1)S(1)}, u32[]{:S(2)}, u32[]{:S(2)}) %collective-permute-start.8) | collective-permute-done | bytes 640032 | tf_op jit(solution)/shard_map/ppermute | solution.py:949
  646.1 13.0 %collective-permute-done.10 = bf16[200,1600]{1,0:T(8,128)(2,1)S(1)} collective-permute-done((bf16[200,1600]{1,0:T(8,128)(2,1)S(1)}, bf16[200,1600]{1,0:T(8,128)(2,1)S(1)}, u32[]{:S(2)}, u32[]{:S(2)}) %collective-permute-start.10) | collective-permute-done | bytes 640032 | tf_op jit(solution)/shard_map/ppermute | solution.py:949
  (181 shorter events, 88.7 us)
Async XLA Ops:
  7.2 54.0 %copy-start.11 = (f32[1,128,1600]{1,2,0:T(8,128)S(1)}, f32[1,128,1600]{1,2,0:T(8,128)}, u32[]{:S(2)}) copy-start(f32[1,128,1600]{1,2,0:T(8,128)} %param.6) | copy-start | bytes 2457604
  7.2 271.3 %all-gather.2.cloned.1.call-start = ((), (), s32[]{:S(2)}) async-start(), calls=%async_computation | async-start | bytes 3833856 | tf_op jit(solution)/shard_map/all_gather | solution.py:1023
  45.9 16.1 %copy-start.12 = (f32[1,128,1600]{1,2,0:T(8,128)S(1)}, f32[1,128,1600]{1,2,0:T(8,128)}, u32[]{:S(2)}) copy-start(f32[1,128,1600]{1,2,0:T(8,128)} %param.11) | copy-start | bytes 2457604
  47.3 140.7 %copy-start.22 = (bf16[1600,128]{0,1:T(8,128)(2,1)}, bf16[1600,128]{0,1:T(8,128)(2,1)S(1)}, u32[]{:S(2)}) copy-start(bf16[1600,128]{0,1:T(8,128)(2,1)S(1)} %broadcast_select_fusion) | copy-start | bytes 1228804
  47.3 140.7 %collective-permute-start.1 = (bf16[1600,128]{0,1:T(8,128)(2,1)S(1)}, bf16[1600,128]{0,1:T(8,128)(2,1)}, u32[]{:S(2)}, u32[]{:S(2)}) collective-permute-start(bf16[1600,128]{0,1:T(8,128)(2,1)S(1)} %broadcast_select_fusion), channel_id=1, source_target_pairs={{0,8},{1,9},{2,10},{3,11},{4,12},{5,13},{6,14},{7,15},{8,0},{9,1},... | collective-permute-start | bytes 1228808 | tf_op jit(solution)/shard_map/ppermute | solution.py:949
  62.3 61.8 %copy-start.5 = (f32[1,128,1600]{2,1,0:T(8,128)}, f32[1,128,1600]{2,1,0:T(8,128)S(1)}, u32[]{:S(2)}) copy-start(f32[1,128,1600]{2,1,0:T(8,128)S(1)} %copy.21) | copy-start | bytes 2457604
  143.2 44.8 %copy-start = (bf16[2048,128]{1,0:T(8,128)(2,1)}, bf16[2048,128]{1,0:T(8,128)(2,1)S(1)}, u32[]{:S(2)}) copy-start(bf16[2048,128]{1,0:T(8,128)(2,1)S(1)} %get-tuple-element.22.o_ref) | copy-start | bytes 1572868
  143.2 46.8 %copy-start.27 = (bf16[1,1024,128]{2,1,0:T(8,128)(2,1)}, bf16[1,1024,128]{2,1,0:T(8,128)(2,1)S(1)}, u32[]{:S(2)}) copy-start(bf16[1,1024,128]{2,1,0:T(8,128)(2,1)S(1)} %get-tuple-element.72) | copy-start | bytes 786436
  143.2 43.0 %collective-permute-start = (bf16[1024,128]{1,0:T(8,128)(2,1)S(1)}, bf16[1024,128]{1,0:T(8,128)(2,1)}, u32[]{:S(2)}, u32[]{:S(2)}) collective-permute-start(bf16[1024,128]{1,0:T(8,128)(2,1)S(1)} %get-tuple-element.73), channel_id=1, source_target_pairs={{0,8},{1,9},{2,10},{3,11},{4,12},{5,13},{6,14},{7,15},{8,0},{9,1},... | collective-permute-start | bytes 786440 | tf_op jit(solution)/shard_map/ppermute | solution.py:949
  144.5 112.2 %collective-permute-start.3 = (bf16[400,1600]{1,0:T(8,128)(2,1)}, bf16[400,1600]{1,0:T(8,128)(2,1)}, u32[]{:S(2)}, u32[]{:S(2)}) collective-permute-start(bf16[400,1600]{1,0:T(8,128)(2,1)} %pad_maximum_fusion.2), channel_id=1, source_target_pairs={{0,16},{16,0},{1,17},{17,1},{2,18},{18,2},{3,19},{19,3},{4,20},{20... | collective-permute-start | bytes 3840008 | tf_op jit(solution)/shard_map/ppermute | solution.py:946
  147.4 84.2 %collective-permute-start.2 = (bf16[400,1600]{1,0:T(8,128)(2,1)}, bf16[400,1600]{1,0:T(8,128)(2,1)}, u32[]{:S(2)}, u32[]{:S(2)}) collective-permute-start(bf16[400,1600]{1,0:T(8,128)(2,1)} %pad_maximum_fusion.2), channel_id=1, source_target_pairs={{0,8},{1,9},{2,10},{3,11},{4,12},{5,13},{6,14},{7,15},{8,0},{9,1},... | collective-permute-start | bytes 3840008 | tf_op jit(solution)/shard_map/ppermute | solution.py:949
  231.7 30.7 %collective-permute-start.4 = (bf16[400,1600]{1,0:T(8,128)(2,1)}, bf16[400,1600]{1,0:T(8,128)(2,1)}, u32[]{:S(2)}, u32[]{:S(2)}) collective-permute-start(bf16[400,1600]{1,0:T(8,128)(2,1)} %collective-permute-done.2), channel_id=1, source_target_pairs={{0,16},{16,0},{1,17},{17,1},{2,18},{18,2},{3,19},{19,3},{4,20},{20... | collective-permute-start | bytes 3840008 | tf_op jit(solution)/shard_map/ppermute | solution.py:946
  258.2 13.3 %copy-start.20 = (bf16[200,1600]{1,0:T(8,128)(2,1)}, bf16[200,1600]{1,0:T(8,128)(2,1)S(1)}, u32[]{:S(2)}) copy-start(bf16[200,1600]{1,0:T(8,128)(2,1)S(1)} %get-tuple-element.65) | copy-start | bytes 1920004
  328.0 270.4 %collective-permute-start.7 = (bf16[400,1600]{1,0:T(8,128)(2,1)}, bf16[400,1600]{1,0:T(8,128)(2,1)}, u32[]{:S(2)}, u32[]{:S(2)}) collective-permute-start(bf16[400,1600]{1,0:T(8,128)(2,1)} %slice.242), channel_id=1, source_target_pairs={{0,16},{16,0},{1,17},{17,1},{2,18},{18,2},{3,19},{19,3},{4,20},{20... | collective-permute-start | bytes 3840008 | tf_op jit(solution)/shard_map/ppermute | solution.py:946
  330.5 22.3 %copy-start.7 = (f32[128,1600]{1,0:T(8,128)S(1)}, f32[128,1600]{1,0:T(8,128)}, u32[]{:S(2)}) copy-start(f32[128,1600]{1,0:T(8,128)} %scatter_cube.4) | copy-start | bytes 2457604
  364.5 25.9 %copy-start.23 = (bf16[1600,128]{0,1:T(8,128)(2,1)S(1)}, bf16[1600,128]{0,1:T(8,128)(2,1)}, u32[]{:S(2)}) copy-start(bf16[1600,128]{0,1:T(8,128)(2,1)} %copy-done.22) | copy-start | bytes 1228804
  365.7 235.4 %collective-permute-start.9 = (bf16[400,1600]{1,0:T(8,128)(2,1)}, bf16[400,1600]{1,0:T(8,128)(2,1)}, u32[]{:S(2)}, u32[]{:S(2)}) collective-permute-start(bf16[400,1600]{1,0:T(8,128)(2,1)} %slice.241), channel_id=1, source_target_pairs={{0,16},{16,0},{1,17},{17,1},{2,18},{18,2},{3,19},{19,3},{4,20},{20... | collective-permute-start | bytes 3840008 | tf_op jit(solution)/shard_map/ppermute | solution.py:946
  393.8 23.8 %collective-permute-start.5 = (bf16[1024,128]{1,0:T(8,128)(2,1)S(1)}, bf16[1024,128]{1,0:T(8,128)(2,1)S(1)}, u32[]{:S(2)}, u32[]{:S(2)}) collective-permute-start(bf16[1024,128]{1,0:T(8,128)(2,1)S(1)} %slice.197), channel_id=1, source_target_pairs={{0,8},{1,9},{2,10},{3,11},{4,12},{5,13},{6,14},{7,15},{8,0},{9,1},... | collective-permute-start | bytes 786440 | tf_op jit(solution)/shard_map/ppermute | solution.py:949
  398.8 19.8 %copy-start.29 = (f32[1600,256]{1,0:T(8,128)}, f32[1600,256]{1,0:T(8,128)S(1)}, u32[]{:S(2)}) copy-start(f32[1600,256]{1,0:T(8,128)S(1)} %fusion.10) | copy-start | bytes 4915204
  399.7 117.9 %collective-permute-start.6 = (bf16[1600,128]{1,0:T(8,128)(2,1)}, bf16[1600,128]{1,0:T(8,128)(2,1)}, u32[]{:S(2)}, u32[]{:S(2)}) collective-permute-start(bf16[1600,128]{1,0:T(8,128)(2,1)} %slice.245), channel_id=1, source_target_pairs={{0,8},{1,9},{2,10},{3,11},{4,12},{5,13},{6,14},{7,15},{8,0},{9,1},... | collective-permute-start | bytes 1228808 | tf_op jit(solution)/shard_map/ppermute | solution.py:949
  499.3 15.4 %copy-start.26 = (bf16[384,1600]{0,1:T(8,128)(2,1)S(1)}, bf16[384,1600]{0,1:T(8,128)(2,1)}, u32[]{:S(2)}) copy-start(bf16[384,1600]{0,1:T(8,128)(2,1)} %convolution_convert_fusion) | copy-start | bytes 3686404
  601.0 43.9 %collective-permute-start.8 = (bf16[200,1600]{1,0:T(8,128)(2,1)S(1)}, bf16[200,1600]{1,0:T(8,128)(2,1)S(1)}, u32[]{:S(2)}, u32[]{:S(2)}) collective-permute-start(bf16[200,1600]{1,0:T(8,128)(2,1)S(1)} %slice.244), channel_id=1, source_target_pairs={{0,8},{1,9},{2,10},{3,11},{4,12},{5,13},{6,14},{7,15},{8,0},{9,1},... | collective-permute-start | bytes 1920008 | tf_op jit(solution)/shard_map/ppermute | solution.py:949
  602.9 56.3 %collective-permute-start.10 = (bf16[200,1600]{1,0:T(8,128)(2,1)S(1)}, bf16[200,1600]{1,0:T(8,128)(2,1)S(1)}, u32[]{:S(2)}, u32[]{:S(2)}) collective-permute-start(bf16[200,1600]{1,0:T(8,128)(2,1)S(1)} %slice.243), channel_id=1, source_target_pairs={{0,8},{1,9},{2,10},{3,11},{4,12},{5,13},{6,14},{7,15},{8,0},{9,1},... | collective-permute-start | bytes 1920008 | tf_op jit(solution)/shard_map/ppermute | solution.py:949
  606.3 54.0 %copy-start.32 = (f32[8,128]{1,0:T(8,128)S(1)}, f32[8,128]{1,0:T(8,128)}, u32[]{:S(2)}) copy-start(f32[8,128]{1,0:T(8,128)} %reduce_vectors.1) | copy-start | bytes 12292
  (24 other events, 128.3 us)
Sparse Core Ops, SparseCore 0:
  124.2 30.0 all-gather.1
